TPU v7x, 256 devices: a whole 4x4x8 slice. The times are simulated.
256 devices in a mesh: group: 8 (over y, core), member: 32 (over x, z).
Axes of the slice: x: 4, y: 4, z: 8, core: 2. Of those that a mesh axis runs over, the one named last changes fastest.
Arguments:
- leaf_solution: bfloat16 [2048, 64, 128], P(('group', 'member')), may hold values from -6 to 6
- leaf_panels: bfloat16 [2048, 3, 4, 128, 128], P(('group', 'member')), may hold values from -0.09375 to 0.09375
- leaf_rows: int32 [2048, 3, 4], P(('group', 'member')), may hold values from 0 to 127, as said below
- sep_panels: bfloat16 [256, 3, 4, 128, 128], P(('group', 'member')), may hold values from -0.25 to 0.25
- sep_rows: int32 [256, 3, 4], P(('group', 'member')), may hold values from 0 to 127, as said below
- right_sides: bfloat16 [3, 256, 64, 128], P(None, ('group', 'member')), may hold values from -6 to 6
- inverse_low: bfloat16 [256, 4096, 128], P(('group', 'member')), may hold values from -0.09375 to 0.09375
- inverse_mid: bfloat16 [256, 8192, 128], P(('group', 'member')), may hold values from -0.0625 to 0.0625
- inverse_top: bfloat16 [256, 16384, 128], P(('group', 'member')), may hold values from -0.046875 to 0.046875
Outputs:
- solution: bfloat16 [3, 256, 64, 128], P(None, ('group', 'member'))
Inputs may be any that keep to these rules, and one draw needn't show every extreme that they name: leaf_rows[k, l, t] is below 32 * 2**l: a block of the ancestor separator at level l; indices may repeat. sep_rows[d, j, t] is below 64, 128, 128 for j = 0, 1, 2: a block of the target separator; indices may repeat.
All inputs are finite; a program needn't handle non-finite values.
Results may differ from a plain program's by a relative error of at most 0.012.
Values may be sent and summed in bfloat16 or wider, within the bound.
No kernel may reach another device: no remote copies, remote signals or barrier semaphores. Data moves between devices by JAX's collectives and lax.ppermute only.
A program may use at most 128 MiB of HBM per device.

v0:
```python
import jax
import jax.numpy as jnp
from jax import lax
from jax.sharding import PartitionSpec as P


def in_blocks(array, dim, devices):
    dims = array.shape
    pieces = array.reshape(*dims[:dim], devices, dims[dim] // devices, *dims[dim + 1 :])
    return jnp.moveaxis(pieces, dim, 0)


def sum_at_owner(array, axis, dim):
    pieces = in_blocks(array, dim, lax.axis_size(axis))
    arrived = lax.all_to_all(pieces, axis, split_axis=0, concat_axis=0, tiled=True)
    return arrived.astype(jnp.float32).sum(axis=0)


def swapped(value, axis, stride):
    mask = 2**stride
    pairs = [(source, source ^ mask) for source in range(lax.axis_size(axis))]
    return lax.ppermute(value, axis, pairs)


def copy_for_each(array, axis):
    devices = lax.axis_size(axis)
    return lax.all_to_all(
        jnp.broadcast_to(array[None], (devices, *array.shape)), axis, 0, 0, tiled=True
    )


def laid_out(pieces, dim):
    pieces = jnp.moveaxis(pieces, 0, dim)
    dims = pieces.shape
    return pieces.reshape(*dims[:dim], dims[dim] * dims[dim + 1], *dims[dim + 2 :])


def collect_2(array, axis, dim):
    pieces = copy_for_each(array, axis)
    return laid_out(pieces, dim)


def spread(terms, rows, blocks):
    count = terms.shape[0]
    onehot = (rows[:, None] == jnp.arange(blocks, dtype=jnp.int32)[None, :]).astype(jnp.float32)
    flat = lax.dot_general(
        onehot, terms.reshape(count, -1), (((0,), (0,)), ((), ())), precision=lax.Precision.HIGHEST
    )
    return flat.reshape(blocks, terms.shape[1], terms.shape[2])


def collect(buffer, level, group_index):
    count = 2**level
    members = buffer.shape[0] // count
    height, width = (buffer.shape[1], buffer.shape[2])
    parts = sum_at_owner(
        buffer.reshape(count, members, height, width).astype(jnp.bfloat16), "member", 1
    )
    parts = parts.reshape(count, height, width)
    if level == 0:
        return parts[0]
    for bit in reversed(range(level)):
        halves = parts.reshape(2, -1, height, width)
        upper = group_index >> bit & 1
        keep = jnp.where(upper == 1, halves[1], halves[0])
        outgoing = jnp.where(upper == 1, halves[0], halves[1])
        parts = keep + swapped(outgoing, "group", bit)
    return parts[0]


def settle(resid, inverse, level, group_index):
    whole = collect_2(resid, "member", 1)
    if level == 0:
        return jnp.dot(whole, inverse, preferred_element_type=jnp.float32).astype(jnp.bfloat16)
    count = 2**level
    width = whole.shape[1]
    held = whole[None]
    for bit in range(level):
        other = swapped(held, "group", bit)
        upper = group_index >> bit & 1
        held = jnp.where(
            upper == 1, jnp.concatenate([other, held], 0), jnp.concatenate([held, other], 0)
        )
    shaped = inverse.reshape(count, width, inverse.shape[1])
    total = jnp.einsum("qrk,qkp->rp", held, shaped, preferred_element_type=jnp.float32)
    return total.astype(jnp.bfloat16)


def on_device(
    leaf_solution,
    leaf_panels,
    leaf_rows,
    sep_panels,
    sep_rows,
    right_sides,
    inverse_low,
    inverse_mid,
    inverse_top,
):
    group_index = lax.axis_index("group")
    members = lax.axis_size("member")
    height, width = (leaf_solution.shape[1], leaf_solution.shape[2])
    terms = jnp.einsum(
        "brp,bltpq->bltrq", leaf_solution, leaf_panels, preferred_element_type=jnp.float32
    )
    leaf_parts = [
        spread(
            terms[:, level].reshape(-1, height, width),
            leaf_rows[:, level].reshape(-1),
            members * 2**level,
        )
        for level in range(3)
    ]
    base_mid = leaf_parts[1]
    base_top = leaf_parts[2]
    resid = (right_sides[0, 0].astype(jnp.float32) - collect(leaf_parts[0], 0, group_index)).astype(
        jnp.bfloat16
    )
    first = settle(resid, inverse_low[0], 0, group_index)
    upward = jnp.einsum(
        "rp,ktpq->ktrq", first, sep_panels[0, :2], preferred_element_type=jnp.float32
    )
    buffer_mid = base_mid + spread(upward[0], sep_rows[0, 0], members * 2)
    resid = (right_sides[1, 0].astype(jnp.float32) - collect(buffer_mid, 1, group_index)).astype(
        jnp.bfloat16
    )
    second = settle(resid, inverse_mid[0], 1, group_index)
    onward = jnp.einsum("rp,tpq->trq", second, sep_panels[0, 2], preferred_element_type=jnp.float32)
    sources = jnp.concatenate([upward[1], onward], 0)
    targets = jnp.concatenate([sep_rows[0, 1], sep_rows[0, 2]], 0)
    buffer_top = base_top + spread(sources, targets, members * 4)
    resid = (right_sides[2, 0].astype(jnp.float32) - collect(buffer_top, 2, group_index)).astype(
        jnp.bfloat16
    )
    third = settle(resid, inverse_top[0], 2, group_index)
    return jnp.stack([first, second, third])[:, None]


def solution(mesh):
    placed = (
        P(("group", "member"), None, None),
        P(("group", "member"), None, None, None, None),
        P(("group", "member"), None, None),
        P(("group", "member"), None, None, None, None),
        P(("group", "member"), None, None),
        P(None, ("group", "member"), None, None),
        P(("group", "member"), None, None),
        P(("group", "member"), None, None),
        P(("group", "member"), None, None),
    )
    return jax.shard_map(
        on_device,
        mesh=mesh,
        in_specs=placed,
        out_specs=P(None, ("group", "member"), None, None),
        check_vma=False,
    )
```

profile of v0, /device:TPU:1, one launch (start us, length us, event | category | flops | bytes accessed | tf_op | source)
XLA Modules:
  0.0 261.5 jit_solution(2579927574984106828)
XLA Ops:
  6.5 26.2 %all_to_all.30 = bf16[32,1,1,64,128]{4,3,2,1,0:T(8,128)(2,1)S(1)} all-to-all(bf16[32,1,1,64,128]{4,3,2,1,0:T(8,128)(2,1)S(1)} %copy.51), channel_id=1, replica_groups=mesh['group'=8,'member'=32] {'member'}, dimensions={0} | all-to-all | bytes 1048576 | tf_op jit(solution)/shard_map/all_to_all | solution.py:15
  34.4 7.4 %all-to-all-start.1 = ((bf16[32,64,128]{2,1,0:T(8,128)(2,1)}), bf16[32,64,128]{2,1,0:T(8,128)(2,1)}, u32[]{:S(2)}, u32[]{:S(2)}) async-start(bf16[32,64,128]{2,1,0:T(8,128)(2,1)} %broadcast_in_dim.12), calls=%async_computation.1 | async-start | bytes 1048576 | tf_op jit(solution)/shard_map/all_to_all | solution.py:27
  42.6 4.2 %fusion.14 = f32[64,64,128]{2,0,1:T(8,128)} fusion(s32[32]{0:T(128)S(1)} %eq.91, f32[4,8,64,128]{3,2,1,0:T(8,128)} %bitcast.184), kind=kOutput, calls=%fused_computation.29 | convolution fusion | flops 201328640 | bytes 3145856 | tf_op jit(solution)/shard_map/dot_general | solution.py:46
  46.8 8.8 %all-to-all-done.1 = bf16[32,64,128]{2,1,0:T(8,128)(2,1)} async-done(((bf16[32,64,128]{2,1,0:T(8,128)(2,1)}), bf16[32,64,128]{2,1,0:T(8,128)(2,1)}, u32[]{:S(2)}, u32[]{:S(2)}) %all-to-all-start.1) | async-done | bytes 524320 | tf_op jit(solution)/shard_map/all_to_all | solution.py:27
  55.6 1.9 convolution_convert_fusion.1
  58.8 2.1 copy.128
  60.9 8.1 %all-to-all-start.2 = ((bf16[32,2,1,64,128]{4,1,3,2,0:T(2,128)(2,1)}), bf16[32,2,1,64,128]{4,1,3,2,0:T(2,128)(2,1)}, u32[]{:S(2)}, u32[]{:S(2)}) async-start(bf16[32,2,1,64,128]{4,1,3,2,0:T(2,128)(2,1)} %bitcast.182), calls=%async_computation.2 | async-start | bytes 2097152 | tf_op jit(solution)/shard_map/all_to_all | solution.py:15
  69.0 25.0 %all-to-all-done.2 = bf16[32,2,1,64,128]{4,1,3,2,0:T(2,128)(2,1)} async-done(((bf16[32,2,1,64,128]{4,1,3,2,0:T(2,128)(2,1)}), bf16[32,2,1,64,128]{4,1,3,2,0:T(2,128)(2,1)}, u32[]{:S(2)}, u32[]{:S(2)}) %all-to-all-start.2) | async-done | bytes 1048608 | tf_op jit(solution)/shard_map/all_to_all | solution.py:15
  95.4 4.9 %collective-permute-start = (f32[1,64,128]{2,0,1:T(1,128)S(1)}, f32[1,64,128]{2,0,1:T(1,128)S(1)}, u32[]{:S(2)}, u32[]{:S(2)}) collective-permute-start(f32[1,64,128]{2,0,1:T(1,128)S(1)} %bitcast.199), channel_id=1, source_target_pairs={{0,32},{32,0},{64,96},{96,64},{128,160},{160,128},{192,224},{224,1... | collective-permute-start | bytes 98312 | tf_op jit(solution)/shard_map/ppermute | solution.py:22
  101.3 18.5 %all_to_all.31 = bf16[32,64,128]{2,1,0:T(8,128)(2,1)S(1)} all-to-all(bf16[32,64,128]{2,1,0:T(8,128)(2,1)S(1)} %broadcast_in_dim.14), channel_id=1, replica_groups=mesh['group'=8,'member'=32] {'member'}, dimensions={0} | all-to-all | bytes 1048576 | tf_op jit(solution)/shard_map/all_to_all | solution.py:27
  121.0 2.1 broadcast_in_dim_reshape.6
  123.1 3.5 %collective-permute-start.1 = (bf16[1,64,4096]{2,1,0:T(8,128)(2,1)}, bf16[1,64,4096]{2,1,0:T(8,128)(2,1)}, u32[]{:S(2)}, u32[]{:S(2)}) collective-permute-start(bf16[1,64,4096]{2,1,0:T(8,128)(2,1)} %broadcast_in_dim_reshape.6), channel_id=1, source_target_pairs={{0,32},{32,0},{64,96},{96,64},{128,160},{160,128},{192,224},{224,1... | collective-permute-start | bytes 1572872 | tf_op jit(solution)/shard_map/ppermute | solution.py:22
  128.5 2.8 %fusion.9 = bf16[64,128]{1,0:T(8,128)(2,1)S(1)} fusion(bf16[2,4096,128]{2,1,0:T(8,128)(2,1)} %bitcast.201, bf16[1,64,4096]{2,1,0:T(8,128)(2,1)} %broadcast_in_dim_reshape.6, bf16[1,64,4096]{2,1,0:T(8,128)(2,1)} %collective-permute-done.1, pred[]{:T(512)S(6)} %eq.90), kind=kOutput, calls=%fused_computation.21 | convolution fusion | flops 135798784 | bytes 3162113 | tf_op jit(solution)/shard_map/qrk,qkp->rp/dot_general | solution.py:85
  132.5 1.9 fusion.28
  134.5 2.6 add_convert_fusion
  137.0 2.4 copy.127
  139.4 5.6 %all-to-all-start.4 = ((bf16[32,4,1,64,128]{4,1,3,2,0:T(4,128)(2,1)}), bf16[32,4,1,64,128]{4,1,3,2,0:T(4,128)(2,1)}, u32[]{:S(2)}, u32[]{:S(2)}) async-start(bf16[32,4,1,64,128]{4,1,3,2,0:T(4,128)(2,1)} %bitcast.180), calls=%async_computation.4 | async-start | bytes 4194304 | tf_op jit(solution)/shard_map/all_to_all | solution.py:15
  145.0 48.8 %all-to-all-done.4 = bf16[32,4,1,64,128]{4,1,3,2,0:T(4,128)(2,1)} async-done(((bf16[32,4,1,64,128]{4,1,3,2,0:T(4,128)(2,1)}), bf16[32,4,1,64,128]{4,1,3,2,0:T(4,128)(2,1)}, u32[]{:S(2)}, u32[]{:S(2)}) %all-to-all-start.4) | async-done | bytes 2097184 | tf_op jit(solution)/shard_map/all_to_all | solution.py:15
  199.0 3.4 %collective-permute-start.3 = (f32[1,64,128]{2,0,1:T(1,128)S(1)}, f32[1,64,128]{2,0,1:T(1,128)S(1)}, u32[]{:S(2)}, u32[]{:S(2)}) collective-permute-start(f32[1,64,128]{2,0,1:T(1,128)S(1)} %broadcast_select_fusion.1), channel_id=1, source_target_pairs={{0,32},{32,0},{64,96},{96,64},{128,160},{160,128},{192,224},{224,1... | collective-permute-start | bytes 98312 | tf_op jit(solution)/shard_map/ppermute | solution.py:22
  203.5 19.9 %all_to_all.32 = bf16[32,64,128]{2,1,0:T(8,128)(2,1)S(1)} all-to-all(bf16[32,64,128]{2,1,0:T(8,128)(2,1)S(1)} %broadcast_in_dim.16), channel_id=1, replica_groups=mesh['group'=8,'member'=32] {'member'}, dimensions={0} | all-to-all | bytes 1048576 | tf_op jit(solution)/shard_map/all_to_all | solution.py:27
  224.6 2.1 broadcast_in_dim_reshape.7
  226.6 3.5 %collective-permute-start.4 = (bf16[1,64,4096]{2,1,0:T(8,128)(2,1)}, bf16[1,64,4096]{2,1,0:T(8,128)(2,1)S(1)}, u32[]{:S(2)}, u32[]{:S(2)}) collective-permute-start(bf16[1,64,4096]{2,1,0:T(8,128)(2,1)} %broadcast_in_dim_reshape.7), channel_id=1, source_target_pairs={{0,32},{32,0},{64,96},{96,64},{128,160},{160,128},{192,224},{224,1... | collective-permute-start | bytes 1572872 | tf_op jit(solution)/shard_map/ppermute | solution.py:22
  234.6 23.0 %collective-permute-done.5 = bf16[2,64,4096]{2,1,0:T(8,128)(2,1)S(1)} collective-permute-done((bf16[2,64,4096]{2,1,0:T(8,128)(2,1)S(1)}, bf16[2,64,4096]{2,1,0:T(8,128)(2,1)S(1)}, u32[]{:S(2)}, u32[]{:S(2)}) %collective-permute-start.5) | collective-permute-done | bytes 1048608 | tf_op jit(solution)/shard_map/ppermute | solution.py:22
  257.7 3.2 %fusion.11 = bf16[1,64,128]{2,1,0:T(8,128)(2,1)S(1)} fusion(bf16[4,4096,128]{2,1,0:T(8,128)(2,1)} %bitcast.200, bf16[2,64,4096]{2,1,0:T(8,128)(2,1)S(1)} %maximum_select_fusion.10, bf16[2,64,4096]{2,1,0:T(8,128)(2,1)S(1)} %collective-permute-done.5, pred[]{:T(512)S(6)} %eq.99), kind=kOutput, calls=%fused_computation.23 | convolution fusion | flops 271589376 | bytes 6307841 | tf_op jit(solution)/shard_map/qrk,qkp->rp/dot_general | solution.py:85
  (67 shorter events, 29.4 us)
Async XLA Ops:
  0.0 1.9 copy-start
  6.3 35.7 %copy-start.7 = (s32[1,3,4]{2,0,1:T(1,128)S(1)}, s32[1,3,4]{2,0,1:T(1,128)}, u32[]{:S(2)}) copy-start(s32[1,3,4]{2,0,1:T(1,128)} %param.13) | copy-start | bytes 148
  34.4 21.2 %all-to-all-start.1 = ((bf16[32,64,128]{2,1,0:T(8,128)(2,1)}), bf16[32,64,128]{2,1,0:T(8,128)(2,1)}, u32[]{:S(2)}, u32[]{:S(2)}) async-start(bf16[32,64,128]{2,1,0:T(8,128)(2,1)} %broadcast_in_dim.12), calls=%async_computation.1 | async-start | bytes 1048576 | tf_op jit(solution)/shard_map/all_to_all | solution.py:27
  42.5 14.9 %copy-start.3 = (bf16[1,3,4,128,128]{4,3,2,1,0:T(8,128)(2,1)S(1)}, bf16[1,3,4,128,128]{4,3,2,1,0:T(8,128)(2,1)}, u32[]{:S(2)}) copy-start(bf16[1,3,4,128,128]{4,3,2,1,0:T(8,128)(2,1)} %param.12) | copy-start | bytes 1179652
  55.6 2.1 copy-start.1
  55.6 2.1 copy-start.6
  60.9 39.4 %copy-start.4 = (bf16[3,1,64,128]{3,2,1,0:T(8,128)(2,1)S(1)}, bf16[3,1,64,128]{3,2,1,0:T(8,128)(2,1)}, u32[]{:S(2)}) copy-start(bf16[3,1,64,128]{3,2,1,0:T(8,128)(2,1)} %param.14) | copy-start | bytes 147460
  60.9 33.2 %all-to-all-start.2 = ((bf16[32,2,1,64,128]{4,1,3,2,0:T(2,128)(2,1)}), bf16[32,2,1,64,128]{4,1,3,2,0:T(2,128)(2,1)}, u32[]{:S(2)}, u32[]{:S(2)}) async-start(bf16[32,2,1,64,128]{4,1,3,2,0:T(2,128)(2,1)} %bitcast.182), calls=%async_computation.2 | async-start | bytes 2097152 | tf_op jit(solution)/shard_map/all_to_all | solution.py:15
  95.3 31.3 %copy-start.5 = (s32[8,1,4]{0,2,1:T(4,128)S(1)}, s32[8,1,4]{0,2,1:T(4,128)}, u32[]{:S(2)}) copy-start(s32[8,1,4]{0,2,1:T(4,128)} %get-tuple-element.16) | copy-start | bytes 388
  95.4 31.4 %copy-start.8 = (s32[4]{0:T(128)S(1)}, s32[4]{0:T(128)}, u32[]{:S(2)}) copy-start(s32[4]{0:T(128)} %get-tuple-element.19) | copy-start | bytes 52
  95.4 31.4 %copy-start.9 = (s32[4]{0:T(128)S(1)}, s32[4]{0:T(128)}, u32[]{:S(2)}) copy-start(s32[4]{0:T(128)} %get-tuple-element.21) | copy-start | bytes 52
  95.4 5.7 %collective-permute-start = (f32[1,64,128]{2,0,1:T(1,128)S(1)}, f32[1,64,128]{2,0,1:T(1,128)S(1)}, u32[]{:S(2)}, u32[]{:S(2)}) collective-permute-start(f32[1,64,128]{2,0,1:T(1,128)S(1)} %bitcast.199), channel_id=1, source_target_pairs={{0,32},{32,0},{64,96},{96,64},{128,160},{160,128},{192,224},{224,1... | collective-permute-start | bytes 98312 | tf_op jit(solution)/shard_map/ppermute | solution.py:22
  123.1 5.4 %collective-permute-start.1 = (bf16[1,64,4096]{2,1,0:T(8,128)(2,1)}, bf16[1,64,4096]{2,1,0:T(8,128)(2,1)}, u32[]{:S(2)}, u32[]{:S(2)}) collective-permute-start(bf16[1,64,4096]{2,1,0:T(8,128)(2,1)} %broadcast_in_dim_reshape.6), channel_id=1, source_target_pairs={{0,32},{32,0},{64,96},{96,64},{128,160},{160,128},{192,224},{224,1... | collective-permute-start | bytes 1572872 | tf_op jit(solution)/shard_map/ppermute | solution.py:22
  132.5 1.9 copy-start.2
  139.4 54.4 %all-to-all-start.4 = ((bf16[32,4,1,64,128]{4,1,3,2,0:T(4,128)(2,1)}), bf16[32,4,1,64,128]{4,1,3,2,0:T(4,128)(2,1)}, u32[]{:S(2)}, u32[]{:S(2)}) async-start(bf16[32,4,1,64,128]{4,1,3,2,0:T(4,128)(2,1)} %bitcast.180), calls=%async_computation.4 | async-start | bytes 4194304 | tf_op jit(solution)/shard_map/all_to_all | solution.py:15
  195.7 3.2 %collective-permute-start.2 = (f32[2,64,128]{2,0,1:T(2,128)S(1)}, f32[2,64,128]{2,0,1:T(2,128)S(1)}, u32[]{:S(2)}, u32[]{:S(2)}) collective-permute-start(f32[2,64,128]{2,0,1:T(2,128)S(1)} %broadcast_select_fusion), channel_id=1, source_target_pairs={{0,64},{32,96},{64,0},{96,32},{128,192},{160,224},{192,128},{224,1... | collective-permute-start | bytes 196616 | tf_op jit(solution)/shard_map/ppermute | solution.py:22
  199.0 4.3 %collective-permute-start.3 = (f32[1,64,128]{2,0,1:T(1,128)S(1)}, f32[1,64,128]{2,0,1:T(1,128)S(1)}, u32[]{:S(2)}, u32[]{:S(2)}) collective-permute-start(f32[1,64,128]{2,0,1:T(1,128)S(1)} %broadcast_select_fusion.1), channel_id=1, source_target_pairs={{0,32},{32,0},{64,96},{96,64},{128,160},{160,128},{192,224},{224,1... | collective-permute-start | bytes 98312 | tf_op jit(solution)/shard_map/ppermute | solution.py:22
  226.6 5.3 %collective-permute-start.4 = (bf16[1,64,4096]{2,1,0:T(8,128)(2,1)}, bf16[1,64,4096]{2,1,0:T(8,128)(2,1)S(1)}, u32[]{:S(2)}, u32[]{:S(2)}) collective-permute-start(bf16[1,64,4096]{2,1,0:T(8,128)(2,1)} %broadcast_in_dim_reshape.7), channel_id=1, source_target_pairs={{0,32},{32,0},{64,96},{96,64},{128,160},{160,128},{192,224},{224,1... | collective-permute-start | bytes 1572872 | tf_op jit(solution)/shard_map/ppermute | solution.py:22
  233.2 24.4 %collective-permute-start.5 = (bf16[2,64,4096]{2,1,0:T(8,128)(2,1)S(1)}, bf16[2,64,4096]{2,1,0:T(8,128)(2,1)S(1)}, u32[]{:S(2)}, u32[]{:S(2)}) collective-permute-start(bf16[2,64,4096]{2,1,0:T(8,128)(2,1)S(1)} %maximum_select_fusion.10), channel_id=1, source_target_pairs={{0,64},{32,96},{64,0},{96,32},{128,192},{160,224},{192,128},{224,1... | collective-permute-start | bytes 3145736 | tf_op jit(solution)/shard_map/ppermute | solution.py:22
where the time goes:
time: 263 us; the launch traced here: 262 us
  waiting for transfers between devices  113 us (43%)
  blocking collectives  64.6 us (25%)
  starting transfers between devices  39.2 us (15%)
  matrix products  21.7 us (8%)
  local copies, waits for them, and re-layouts  16.9 us (6%)
  other arithmetic  6.32 us (2%)
    all_to_all x2, waiting for transfers between devices, sum_at_owner(): lax.all_to_all(pieces, axis, split_axis=0, concat_axis=0, tiled=True)  73.8 us
    all_to_all x2, blocking collectives, copy_for_each(): lax.all_to_all(jnp.broadcast_to(array[None], (devices, *array.shape)), ax...  38.4 us
    ppermute x6, waiting for transfers between devices, swapped(): return lax.ppermute(value, axis, pairs)  30 us
    all_to_all x1, blocking collectives, sum_at_owner(): lax.all_to_all(pieces, axis, split_axis=0, concat_axis=0, tiled=True)  26.2 us
    ppermute x6, starting transfers between devices, swapped(): return lax.ppermute(value, axis, pairs)  18.1 us
    all_to_all x2, starting transfers between devices, sum_at_owner(): lax.all_to_all(pieces, axis, split_axis=0, concat_axis=0, tiled=True)  13.7 us
    dot_general x5, matrix products, spread(): lax.dot_general(onehot, terms.reshape(count, -1), (((0,), (0,)), ((), ())...  11.1 us
    all_to_all x1, waiting for transfers between devices, copy_for_each(): lax.all_to_all(jnp.broadcast_to(array[None], (devices, *array.shape)), ax...  8.77 us
  transfers between devices with their start and end apart: 9, of which 9 were waited for; matrix products, arithmetic and copies ran while one was open for 2% of the time, Pallas kernels for 0%

commit v1 on v0

v1 whole, which is shorter than its diff:
```python
import functools

import jax
import jax.numpy as jnp
from jax import lax
from jax.experimental import pallas as pl
from jax.experimental.pallas import tpu as pltpu
from jax.sharding import PartitionSpec as P

ALONG_X = 4
DEPTH = 8
BF16 = jnp.bfloat16
F32 = jnp.float32
WHOLE = pl.BlockSpec(memory_space=pltpu.VMEM)
SCALARS = pl.BlockSpec(memory_space=pltpu.SMEM)
PARAMS = pltpu.CompilerParams(vmem_limit_bytes=40 * 2**20)


def slot(entry, place):
    x = place[0]
    z = lax.rem(entry, DEPTH)
    step = (lax.div(entry, DEPTH) + (ALONG_X - x)) & (ALONG_X - 1)
    return lax.rem(step, ALONG_X) * DEPTH + z


def slot_at(entry, place, level):
    members = ALONG_X * DEPTH
    inner = slot(lax.rem(entry, members), place)
    group = lax.div(entry, members)
    core = (group & 1) ^ place[1]
    if level == 0:
        return inner
    if level == 1:
        return core * members + inner
    high = (lax.div(group, 2) & 1) ^ place[2]
    return core * (2 * members) + high * members + inner


def leaf_kernel(level, place, rows, values, panels, out, total):
    blocks = out.shape[0]
    count, targets = panels.shape[0], panels.shape[2]

    @pl.loop(0, blocks // 8)
    def _(i):
        total[pl.ds(i * 8, 8)] = jnp.zeros((8, *total.shape[1:]), F32)

    for k in range(count):
        value = values[k]
        for t in range(targets):
            at = slot_at(rows[k * 12 + level * 4 + t], place, level)
            total[at] += jnp.dot(value, panels[k, 0, t], preferred_element_type=F32)

    @pl.loop(0, blocks // 8)
    def _(i):
        out[pl.ds(i * 8, 8)] = total[pl.ds(i * 8, 8)].astype(BF16)


def leaf_sums(level, place, rows, values, panels):
    count, levels, targets, p, q = panels.shape
    height = values.shape[1]
    blocks = ALONG_X * DEPTH * 2**level
    return pl.pallas_call(
        functools.partial(leaf_kernel, level),
        grid=(1,),
        in_specs=[
            SCALARS,
            SCALARS,
            pl.BlockSpec((count, height, p), lambda i: (0, 0, 0)),
            pl.BlockSpec((count, 1, targets, p, q), lambda i: (0, level, 0, 0, 0)),
        ],
        out_specs=pl.BlockSpec((blocks, height, q), lambda i: (0, 0, 0)),
        out_shape=jax.ShapeDtypeStruct((blocks, height, q), BF16),
        scratch_shapes=[pltpu.VMEM((blocks, height, q), F32)],
        compiler_params=PARAMS,
        cost_estimate=pl.CostEstimate(
            flops=2 * count * targets * height * p * q,
            bytes_accessed=2 * count * targets * p * q + 2 * blocks * height * q,
            transcendentals=0,
        ),
        name=f"leaf{level}",
    )(place, rows, values, panels)


def partial_kernel(sets, place, p0, p1, p2, p3, *refs):
    weights, outs = refs[:sets], refs[sets:]
    sums = [None] * sets
    depth = DEPTH * 128
    for k, part in enumerate((p0, p1, p2, p3)):
        lhs = jnp.concatenate([part[z] for z in range(DEPTH)], axis=1)
        start = pl.multiple_of(((place[0] + ALONG_X - k) & (ALONG_X - 1)) * depth, depth)
        for s in range(sets):
            term = jnp.dot(lhs, weights[s][0, pl.ds(start, depth), :], preferred_element_type=F32)
            sums[s] = term if sums[s] is None else sums[s] + term
    for s in range(sets):
        outs[s][...] = sums[s].astype(outs[s].dtype)


def partials(place, parts, inverse, others, kind):
    rows, columns = ALONG_X * DEPTH * 128, inverse.shape[-1]
    height = parts[0].shape[1]
    sets = 1 + len(others)
    fixed = lambda *dims: pl.BlockSpec(dims, lambda i, q: (0,) * len(dims))
    return pl.pallas_call(
        functools.partial(partial_kernel, sets),
        grid_spec=pltpu.PrefetchScalarGridSpec(
            num_scalar_prefetch=1,
            grid=(1,),
            in_specs=[fixed(*parts[0].shape)] * 4
            + [pl.BlockSpec((1, rows, columns), lambda i, q: (0, q[3] if sets > 1 else 0, 0))]
            + [fixed(1, rows, columns)] * (sets - 1),
            out_specs=[fixed(height, columns)] * sets,
        ),
        out_shape=[jax.ShapeDtypeStruct((height, columns), kind)] * sets,
        compiler_params=PARAMS,
        cost_estimate=pl.CostEstimate(
            flops=2 * sets * height * rows * columns,
            bytes_accessed=2 * sets * rows * columns,
            transcendentals=0,
        ),
        name=f"settle{sets}",
    )(place, *parts, inverse, *others)


def add_kernel(level, pair, place, rows, value, panels, base, keep, send):
    half = keep.shape[0]

    @pl.loop(0, half // 8)
    def _(i):
        keep[pl.ds(i * 8, 8)] = base[pl.ds(i * 8, 8)]
        send[pl.ds(i * 8, 8)] = base[pl.ds(half + i * 8, 8)]

    lhs = value[...]
    for t in range(panels.shape[2]):
        at = slot_at(rows[pair * 4 + t], place, level)
        term = jnp.dot(lhs, panels[0, 0, t], preferred_element_type=F32)

        @pl.when(at < half)
        def _():
            keep[at] = (keep[at].astype(F32) + term).astype(BF16)

        @pl.when(at >= half)
        def _():
            send[at - half] = (send[at - half].astype(F32) + term).astype(BF16)


def add_terms(level, pair, place, rows, value, panels, base):
    blocks, height, columns = base.shape
    targets, p = panels.shape[2:4]
    half = jax.ShapeDtypeStruct((blocks // 2, height, columns), BF16)
    fixed = lambda *dims: pl.BlockSpec(dims, lambda i: (0,) * len(dims))
    return pl.pallas_call(
        functools.partial(add_kernel, level, pair),
        grid=(1,),
        in_specs=[
            SCALARS,
            SCALARS,
            fixed(height, p),
            pl.BlockSpec((1, 1, targets, p, columns), lambda i: (0, pair, 0, 0, 0)),
            fixed(*base.shape),
        ],
        out_specs=[fixed(*half.shape)] * 2,
        out_shape=[half, half],
        compiler_params=PARAMS,
        cost_estimate=pl.CostEstimate(
            flops=2 * targets * height * p * columns,
            bytes_accessed=4 * blocks * height * columns,
            transcendentals=0,
        ),
        name=f"add{level}",
    )(place, rows, value, panels, base)


def pieces_kernel(parts, a, b, *outs):
    each = a.shape[0] // parts

    for k in range(parts):

        @pl.loop(0, each // 8)
        def _(i):
            at = pl.ds(k * each + i * 8, 8)
            outs[k][pl.ds(i * 8, 8)] = (a[at].astype(F32) + b[at].astype(F32)).astype(BF16)


def sum_in_pieces(a, b, parts):
    piece = jax.ShapeDtypeStruct((a.shape[0] // parts, *a.shape[1:]), BF16)
    return pl.pallas_call(
        functools.partial(pieces_kernel, parts),
        in_specs=[WHOLE] * 2,
        out_specs=[WHOLE] * parts,
        out_shape=[piece] * parts,
        compiler_params=PARAMS,
        cost_estimate=pl.CostEstimate(flops=a.size, bytes_accessed=6 * a.size, transcendentals=0),
        name=f"pieces{parts}",
    )(a, b)


def terms_kernel(mine, other, panels, out, solution):
    solved = (mine[...] + other[...]).astype(BF16)
    solution[...] = solved
    for t in range(panels.shape[2]):
        out[t] = jnp.dot(solved, panels[0, 0, t], preferred_element_type=F32).astype(BF16)


def solve_and_terms(mine, other, panels, pair):
    height, columns = mine.shape
    targets, p = panels.shape[2:4]
    fixed = lambda *dims: pl.BlockSpec(dims, lambda i: (0,) * len(dims))
    return pl.pallas_call(
        terms_kernel,
        grid=(1,),
        in_specs=[
            fixed(height, columns),
            fixed(height, columns),
            pl.BlockSpec((1, 1, targets, p, columns), lambda i: (0, pair, 0, 0, 0)),
        ],
        out_specs=[fixed(targets, height, columns), fixed(height, columns)],
        out_shape=[
            jax.ShapeDtypeStruct((targets, height, columns), BF16),
            jax.ShapeDtypeStruct((height, columns), BF16),
        ],
        compiler_params=PARAMS,
        cost_estimate=pl.CostEstimate(
            flops=2 * targets * height * p * columns,
            bytes_accessed=4 * targets * p * columns,
            transcendentals=0,
        ),
        name="terms",
    )(mine, other, panels)


def merge_kernel(place, rows, a, b, *refs):
    terms, outs, total = refs[:4], refs[4:8], refs[8]
    blocks = a.shape[0]
    members = ALONG_X * DEPTH

    @pl.loop(0, blocks // 8)
    def _(i):
        at = pl.ds(i * 8, 8)
        total[at] = a[at].astype(F32) + b[at].astype(F32)

    for source, term in enumerate(terms):
        for t in range(term.shape[0]):
            entry = rows[source * 4 + t]

            @pl.when(lax.div(entry, members) == place[3])
            def _():
                at = slot(lax.rem(entry, members), place)
                total[at] += term[t].astype(F32)

    for k in range(ALONG_X):
        outs[k][...] = total[pl.ds(k * DEPTH, DEPTH)].astype(BF16)


def merge(place, rows, a, b, terms):
    piece = jax.ShapeDtypeStruct((DEPTH, *a.shape[1:]), BF16)
    return pl.pallas_call(
        merge_kernel,
        in_specs=[SCALARS] * 2 + [WHOLE] * 6,
        out_specs=[WHOLE] * ALONG_X,
        out_shape=[piece] * ALONG_X,
        scratch_shapes=[pltpu.VMEM(a.shape, F32)],
        compiler_params=PARAMS,
        cost_estimate=pl.CostEstimate(flops=a.size, bytes_accessed=6 * a.size, transcendentals=0),
        name="merge",
    )(place, rows, a, b, *terms)


def along_x(value, step):
    pairs = [
        (x * DEPTH + z, (x + step) % ALONG_X * DEPTH + z)
        for x in range(ALONG_X)
        for z in range(DEPTH)
    ]
    return lax.ppermute(value, "member", pairs)


def swapped(value, mask):
    return lax.ppermute(value, "group", [(g, g ^ mask) for g in range(lax.axis_size("group"))])


def over_z(pieces):
    groups = [[x * DEPTH + z for z in range(DEPTH)] for x in range(ALONG_X)]
    return lax.all_to_all(pieces, "member", 0, 0, axis_index_groups=groups, tiled=True)


def collect(pieces, right):
    arrived = [along_x(pieces[k], k) for k in (2, 1, 3)]
    total = pieces[0].astype(F32)
    for part in arrived:
        total = total + part.astype(F32)
    summed = over_z(total.astype(BF16))
    return (right.astype(F32) - summed.astype(F32).sum(axis=0)).astype(BF16)


def gather(resid):
    own = over_z(jnp.broadcast_to(resid[None], (DEPTH, *resid.shape)))
    far = along_x(own, 2)
    near = [along_x(own, k) for k in (1, 3)]
    return own, near[0], far, near[1]


def on_device(
    leaf_solution,
    leaf_panels,
    leaf_rows,
    sep_panels,
    sep_rows,
    right_sides,
    inverse_low,
    inverse_mid,
    inverse_top,
):
    group = lax.axis_index("group").astype(jnp.int32)
    member = lax.axis_index("member").astype(jnp.int32)
    core, high = group & 1, group >> 1 & 1
    quarter = group & 3
    x = member // DEPTH
    place_mid = jnp.stack([x, core, high, core])
    place = jnp.stack([x, core, high, quarter])
    rows = leaf_rows.reshape(-1)
    source = sep_rows.reshape(-1)
    span = ALONG_X * DEPTH * inverse_low.shape[-1]

    def turned(inverse, count, at):
        return lax.dynamic_slice_in_dim(inverse, at * span, span, 1)

    mid_other = swapped(turned(inverse_mid, 2, core ^ 1), 1)
    top_others = [swapped(turned(inverse_top, 4, quarter ^ mask), mask) for mask in (1, 2, 3)]
    rows_mine = source[8:12]
    rows_high = swapped(rows_mine, 2)
    rows_two = jnp.concatenate([rows_mine, rows_high])
    rows_all = jnp.concatenate([rows_two, swapped(rows_two, 1)])

    base_low = leaf_sums(0, place, rows, leaf_solution, leaf_panels)
    base_mid = leaf_sums(1, place, rows, leaf_solution, leaf_panels)
    base_top = leaf_sums(2, place, rows, leaf_solution, leaf_panels)

    resid = collect([base_low[k * DEPTH : (k + 1) * DEPTH] for k in range(ALONG_X)], right_sides[0, 0])
    (first,) = partials(place, gather(resid), inverse_low, [], BF16)

    keep, send = add_terms(1, 0, place, source, first, sep_panels, base_mid)
    resid = collect(sum_in_pieces(keep, swapped(send, 1), ALONG_X), right_sides[1, 0])

    keep_top, send_top = add_terms(2, 1, place, source, first, sep_panels, base_top)
    stay, leave = sum_in_pieces(keep_top, swapped(send_top, 1), 2)
    arrived = swapped(leave, 2)

    mine, theirs = partials(place_mid, gather(resid), inverse_mid, [mid_other], F32)
    terms, second = solve_and_terms(mine, swapped(theirs, 1), sep_panels, 2)
    terms_high = swapped(terms, 2)
    terms_core = swapped(terms, 1)
    terms_both = swapped(terms_high, 1)
    pieces = merge(place, rows_all, stay, arrived, [terms, terms_high, terms_core, terms_both])
    resid = collect(pieces, right_sides[2, 0])
    mine, by_core, by_high, by_both = partials(place, gather(resid), inverse_top, top_others, F32)
    pair = swapped(jnp.stack([by_high, by_both]), 2)
    third = (mine + pair[0] + swapped(by_core + pair[1], 1)).astype(BF16)
    return jnp.stack([first, second, third])[:, None]


def solution(mesh):
    placed = (
        P(("group", "member"), None, None),
        P(("group", "member"), None, None, None, None),
        P(("group", "member"), None, None),
        P(("group", "member"), None, None, None, None),
        P(("group", "member"), None, None),
        P(None, ("group", "member"), None, None),
        P(("group", "member"), None, None),
        P(("group", "member"), None, None),
        P(("group", "member"), None, None),
    )
    return jax.shard_map(
        on_device,
        mesh=mesh,
        in_specs=placed,
        out_specs=P(None, ("group", "member"), None, None),
        check_vma=False,
    )
```

time: 263 us -> 185 us (0.70)
  waiting for transfers between devices: 113 us -> 44.6 us
  matrix products: 21.7 us -> 0 us
  Pallas kernels: 0 us -> 13.9 us
  local copies, waits for them, and re-layouts: 16.9 us -> 12.4 us
  starting transfers between devices: 39.2 us -> 42.4 us
    all_to_all x3 -> x0, waiting for transfers between devices: 82.6 us -> none  [the longest x2 73.8 us: sum_at_owner(): lax.all_to_all(pieces, axis, split_axis=0, concat_axis=0, tiled=True)]
    ppermute x6 -> x33, starting transfers between devices: 18.1 us -> 42.4 us  [the longest x15 21.8 us: swapped(): lax.ppermute(value, 'group', [(g, g ^ mask) for g in range(lax.axis_size(...]
    dot_general x11 -> x0, matrix products: 21.7 us -> none  [the longest x5 11.1 us: spread(): lax.dot_general(onehot, terms.reshape(count, -1), (((0,), (0,)), ((), ())...]
    all_to_all x3 -> x0, starting transfers between devices: 21.1 us -> none  [the longest x2 13.7 us: sum_at_owner(): lax.all_to_all(pieces, axis, split_axis=0, concat_axis=0, tiled=True)]
    ppermute x6 -> x33, waiting for transfers between devices: 30 us -> 44.6 us  [the longest x15 30.4 us: swapped(): lax.ppermute(value, 'group', [(g, g ^ mask) for g in range(lax.axis_size(...]
    pallas_call x0 -> x12, Pallas kernels: none -> 13.9 us  [the longest x3 4.33 us: partials(): pl.pallas_call(functools.partial(partial_kernel, sets), grid_spec=pltpu.P...]
    unnamed x23 -> x45, local copies, waits for them, and re-layouts: 0.4 us -> 7.63 us
    convert_element_type x2 -> x0, local copies, waits for them, and re-layouts: 4.45 us -> none  [collect(): buffer.reshape(count, members, height, width).astype(jnp.bfloat16)]
  transfers between devices with their start and end apart: 9 -> 33, of which waited for: 9 -> 17; matrix products, arithmetic and copies ran while one was open for 2% -> 4% of each run, Pallas kernels for 0% -> 3%
where the time goes in v1:
time: 185 us; the launch traced here: 184 us
  blocking collectives  66.5 us (36%)
  waiting for transfers between devices  44.6 us (24%)
  starting transfers between devices  42.4 us (23%)
  Pallas kernels  13.9 us (8%)
  local copies, waits for them, and re-layouts  12.4 us (7%)
  other arithmetic  4.01 us (2%)
    all_to_all x6, blocking collectives, over_z(): lax.all_to_all(pieces, 'member', 0, 0, axis_index_groups=groups, tiled=True)  66.5 us
    ppermute x15, waiting for transfers between devices, swapped(): lax.ppermute(value, 'group', [(g, g ^ mask) for g in range(lax.axis_size(...  30.4 us
    ppermute x15, starting transfers between devices, swapped(): lax.ppermute(value, 'group', [(g, g ^ mask) for g in range(lax.axis_size(...  21.8 us
    ppermute x18, starting transfers between devices, along_x(): return lax.ppermute(value, 'member', pairs)  20.6 us
    ppermute x18, waiting for transfers between devices, along_x(): return lax.ppermute(value, 'member', pairs)  14.2 us
    unnamed x45, local copies, waits for them, and re-layouts  7.63 us
    pallas_call x3, Pallas kernels, partials(): pl.pallas_call(functools.partial(partial_kernel, sets), grid_spec=pltpu.P...  4.33 us
    pallas_call x3, Pallas kernels, leaf_sums(): pl.pallas_call(functools.partial(leaf_kernel, level), grid=(1,), in_specs...  3.83 us
  transfers between devices with their start and end apart: 33, of which 17 were waited for; matrix products, arithmetic and copies ran while one was open for 4% of the time, Pallas kernels for 3%

profile of v1, /device:TPU:1, one launch (start us, length us, event | category | flops | bytes accessed | tf_op | source)
XLA Modules:
  0.0 184.1 jit_solution(8985911508511683466)
XLA Ops:
  1.6 1.9 %copy-done = bf16[8,3,4,128,128]{4,3,2,1,0:T(8,128)(2,1)S(1)} copy-done((bf16[8,3,4,128,128]{4,3,2,1,0:T(8,128)(2,1)S(1)}, bf16[8,3,4,128,128]{4,3,2,1,0:T(8,128)(2,1)}, u32[]{:S(2)}) %copy-start) | copy-done | bytes 3145752
  5.6 3.6 %collective-permute-start = (bf16[8,64,128]{2,1,0:T(8,128)(2,1)S(1)}, bf16[8,64,128]{2,1,0:T(8,128)(2,1)S(1)}, u32[]{:S(2)}, u32[]{:S(2)}) collective-permute-start(bf16[8,64,128]{2,1,0:T(8,128)(2,1)S(1)} %get-tuple-element.54), channel_id=1, source_target_pairs={{0,16},{1,17},{2,18},{3,19},{4,20},{5,21},{6,22},{7,23},{8,24},{9,... | collective-permute-start | bytes 393224 | tf_op jit(solution)/shard_map/ppermute | solution.py:274
  11.6 3.7 %collective-permute-done.2 = bf16[8,64,128]{2,1,0:T(8,128)(2,1)S(1)} collective-permute-done((bf16[8,64,128]{2,1,0:T(8,128)(2,1)S(1)}, bf16[8,64,128]{2,1,0:T(8,128)(2,1)S(1)}, u32[]{:S(2)}, u32[]{:S(2)}) %collective-permute-start.2) | collective-permute-done | bytes 131104 | tf_op jit(solution)/shard_map/ppermute | solution.py:274
  15.3 2.2 %collective-permute-done.1 = bf16[8,64,128]{2,1,0:T(8,128)(2,1)S(1)} collective-permute-done((bf16[8,64,128]{2,1,0:T(8,128)(2,1)S(1)}, bf16[8,64,128]{2,1,0:T(8,128)(2,1)S(1)}, u32[]{:S(2)}, u32[]{:S(2)}) %collective-permute-start.1) | collective-permute-done | bytes 131104 | tf_op jit(solution)/shard_map/ppermute | solution.py:274
  17.5 13.9 %all_to_all.30 = bf16[8,64,128]{2,1,0:T(8,128)(2,1)S(1)} all-to-all(bf16[8,64,128]{2,1,0:T(8,128)(2,1)S(1)} %add_convert_fusion.2), channel_id=1, replica_groups={{0,1,2,3,4,5,6,7},{8,9,10,11,12,13,14,15},{16,17,18,19,20,21,22,23},{24..., dimensions={0} | all-to-all | bytes 262144 | tf_op jit(solution)/shard_map/all_to_all | solution.py:283
  32.2 11.1 %all_to_all.31.p0 = bf16[8,64,128]{2,1,0:T(8,128)(2,1)} all-to-all(bf16[8,64,128]{2,1,0:T(8,128)(2,1)S(1)} %broadcast_in_dim.8), channel_id=1, replica_groups={{0,1,2,3,4,5,6,7},{8,9,10,11,12,13,14,15},{16,17,18,19,20,21,22,23},{24..., dimensions={0} | all-to-all | bytes 262144 | tf_op jit(solution)/shard_map/all_to_all | solution.py:283
  43.3 3.0 %collective-permute-start.5 = (bf16[8,64,128]{2,1,0:T(8,128)(2,1)}, bf16[8,64,128]{2,1,0:T(8,128)(2,1)}, u32[]{:S(2)}, u32[]{:S(2)}) collective-permute-start(bf16[8,64,128]{2,1,0:T(8,128)(2,1)} %all_to_all.31.p0), channel_id=1, source_target_pairs={{0,24},{1,25},{2,26},{3,27},{4,28},{5,29},{6,30},{7,31},{8,0},{9,1... | collective-permute-start | bytes 393224 | tf_op jit(solution)/shard_map/ppermute | solution.py:274
  50.2 1.8 collective-permute-done.4.p2
  54.0 2.0 %settle1.1.value = bf16[64,128]{1,0:T(8,128)(2,1)S(1)} custom-call(s32[4]{0:T(128)S(1)} %copy-done.12, bf16[8,64,128]{2,1,0:T(8,128)(2,1)} %all_to_all.31.p0, bf16[8,64,128]{2,1,0:T(8,128)(2,1)} %collective-permute-done.3.p1, bf16[8,64,128]{2,1,0:T(8,128)(2,1)} %collective-permute-done.4.p2, bf16[8,64,128]{2,1,0:T(8,128)(2,1)} %collective-permute-done.5.p3, ...), custom_call_target="tpu_custom_call" | custom-call | flops 67108864 | bytes 1048576 | tf_op jit(solution)/shard_map/settle1/pallas_call | solution.py:103
  56.6 2.0 %add1.1 = (bf16[32,64,128]{2,1,0:T(8,128)(2,1)S(1)}, bf16[32,64,128]{2,1,0:T(8,128)(2,1)}) custom-call(s32[4]{0:T(128)S(1)} %copy-done.13, s32[12]{0:T(128)S(1)} %copy-done.18, bf16[64,128]{1,0:T(8,128)(2,1)S(1)} %settle1.1.value, bf16[1,3,4,128,128]{4,3,2,1,0:T(8,128)(2,1)S(1)} %copy-done.4, bf16[64,64,128]{2,1,0:T(8,128)(2,1)S(1)} %leaf1.1.base), custom_call_target="tpu_custom_call" | custom-call | flops 8388608 | bytes 2097152 | tf_op jit(solution)/shard_map/add1/pallas_call | solution.py:151
  59.4 4.8 %collective-permute-start.6 = (bf16[32,64,128]{2,1,0:T(8,128)(2,1)}, bf16[32,64,128]{2,1,0:T(8,128)(2,1)}, u32[]{:S(2)}, u32[]{:S(2)}) collective-permute-start(bf16[32,64,128]{2,1,0:T(8,128)(2,1)} %get-tuple-element.28), channel_id=1, source_target_pairs={{0,32},{32,0},{64,96},{96,64},{128,160},{160,128},{192,224},{224,1... | collective-permute-start | bytes 1572872 | tf_op jit(solution)/shard_map/ppermute | solution.py:278
  64.1 1.9 %collective-permute-done.6.b = bf16[32,64,128]{2,1,0:T(8,128)(2,1)} collective-permute-done((bf16[32,64,128]{2,1,0:T(8,128)(2,1)}, bf16[32,64,128]{2,1,0:T(8,128)(2,1)}, u32[]{:S(2)}, u32[]{:S(2)}) %collective-permute-start.6) | collective-permute-done | bytes 524320 | tf_op jit(solution)/shard_map/ppermute | solution.py:278
  69.2 2.5 %collective-permute-start.9 = (bf16[8,64,128]{2,1,0:T(8,128)(2,1)S(1)}, bf16[8,64,128]{2,1,0:T(8,128)(2,1)S(1)}, u32[]{:S(2)}, u32[]{:S(2)}) collective-permute-start(bf16[8,64,128]{2,1,0:T(8,128)(2,1)S(1)} %get-tuple-element.32), channel_id=1, source_target_pairs={{0,24},{1,25},{2,26},{3,27},{4,28},{5,29},{6,30},{7,31},{8,0},{9,1... | collective-permute-start | bytes 393224 | tf_op jit(solution)/shard_map/ppermute | solution.py:274
  78.1 10.6 %all_to_all.32 = bf16[8,64,128]{2,1,0:T(8,128)(2,1)S(1)} all-to-all(bf16[8,64,128]{2,1,0:T(8,128)(2,1)S(1)} %add_convert_fusion.1), channel_id=1, replica_groups={{0,1,2,3,4,5,6,7},{8,9,10,11,12,13,14,15},{16,17,18,19,20,21,22,23},{24..., dimensions={0} | all-to-all | bytes 262144 | tf_op jit(solution)/shard_map/all_to_all | solution.py:283
  89.5 10.3 %all_to_all.33.p0 = bf16[8,64,128]{2,1,0:T(8,128)(2,1)S(1)} all-to-all(bf16[8,64,128]{2,1,0:T(8,128)(2,1)S(1)} %broadcast_in_dim.9), channel_id=1, replica_groups={{0,1,2,3,4,5,6,7},{8,9,10,11,12,13,14,15},{16,17,18,19,20,21,22,23},{24..., dimensions={0} | all-to-all | bytes 262144 | tf_op jit(solution)/shard_map/all_to_all | solution.py:283
  107.6 4.8 %collective-permute-start.14 = (f32[64,128]{1,0:T(8,128)S(1)}, f32[64,128]{1,0:T(8,128)S(1)}, u32[]{:S(2)}, u32[]{:S(2)}) collective-permute-start(f32[64,128]{1,0:T(8,128)S(1)} %get-tuple-element.34), channel_id=1, source_target_pairs={{0,32},{32,0},{64,96},{96,64},{128,160},{160,128},{192,224},{224,1... | collective-permute-start | bytes 98312 | tf_op jit(solution)/shard_map/ppermute | solution.py:278
  120.9 1.9 %collective-permute-start.22 = (bf16[8,64,128]{2,1,0:T(8,128)(2,1)S(1)}, bf16[8,64,128]{2,1,0:T(8,128)(2,1)S(1)}, u32[]{:S(2)}, u32[]{:S(2)}) collective-permute-start(bf16[8,64,128]{2,1,0:T(8,128)(2,1)S(1)} %get-tuple-element.42), channel_id=1, source_target_pairs={{0,16},{1,17},{2,18},{3,19},{4,20},{5,21},{6,22},{7,23},{8,24},{9,... | collective-permute-start | bytes 393224 | tf_op jit(solution)/shard_map/ppermute | solution.py:274
  122.9 2.7 %collective-permute-start.24 = (bf16[8,64,128]{2,1,0:T(8,128)(2,1)S(1)}, bf16[8,64,128]{2,1,0:T(8,128)(2,1)S(1)}, u32[]{:S(2)}, u32[]{:S(2)}) collective-permute-start(bf16[8,64,128]{2,1,0:T(8,128)(2,1)S(1)} %get-tuple-element.44), channel_id=1, source_target_pairs={{0,24},{1,25},{2,26},{3,27},{4,28},{5,29},{6,30},{7,31},{8,0},{9,1... | collective-permute-start | bytes 393224 | tf_op jit(solution)/shard_map/ppermute | solution.py:274
  125.5 2.1 %constant_dynamic-slice_fusion = (bf16[1,4096,128]{2,1,0:T(8,128)(2,1)S(1)}, bf16[1,4096,128]{2,1,0:T(8,128)(2,1)S(1)}, bf16[1,4096,128]{2,1,0:T(8,128)(2,1)S(1)}) fusion(bf16[1,16384,128]{2,1,0:T(8,128)(2,1)} %refs_0_.5, s32[]{:T(128)S(6)} %select_n.21, s32[]{:T(128)S(6)} %select_n.20, s32[]{:T(128)S(6)} %select_n.19), kind=kLoop, calls=%fused_computation.21 | loop fusion | bytes 6291468 | tf_op jit(solution)/shard_map/dynamic_slice | solution.py:325
  127.6 2.5 %collective-permute-start.30 = (bf16[1,4096,128]{2,1,0:T(8,128)(2,1)S(1)}, bf16[1,4096,128]{2,1,0:T(8,128)(2,1)S(1)}, u32[]{:S(2)}, u32[]{:S(2)}) collective-permute-start(bf16[1,4096,128]{2,1,0:T(8,128)(2,1)S(1)} %get-tuple-element.51), channel_id=1, source_target_pairs={{0,96},{32,64},{64,32},{96,0},{128,224},{160,192},{192,160},{224,1... | collective-permute-start | bytes 3145736 | tf_op jit(solution)/shard_map/ppermute | solution.py:278
  130.7 10.2 %all_to_all.34 = bf16[8,64,128]{2,1,0:T(8,128)(2,1)S(1)} all-to-all(bf16[8,64,128]{2,1,0:T(8,128)(2,1)S(1)} %add_convert_fusion), channel_id=1, replica_groups={{0,1,2,3,4,5,6,7},{8,9,10,11,12,13,14,15},{16,17,18,19,20,21,22,23},{24..., dimensions={0} | all-to-all | bytes 262144 | tf_op jit(solution)/shard_map/all_to_all | solution.py:283
  141.7 10.4 %all_to_all.35.p0 = bf16[8,64,128]{2,1,0:T(8,128)(2,1)S(1)} all-to-all(bf16[8,64,128]{2,1,0:T(8,128)(2,1)S(1)} %broadcast_in_dim.10), channel_id=1, replica_groups={{0,1,2,3,4,5,6,7},{8,9,10,11,12,13,14,15},{16,17,18,19,20,21,22,23},{24..., dimensions={0} | all-to-all | bytes 262144 | tf_op jit(solution)/shard_map/all_to_all | solution.py:283
  154.1 22.2 %collective-permute-done.29.refs_2_ = bf16[1,4096,128]{2,1,0:T(8,128)(2,1)S(1)} collective-permute-done((bf16[1,4096,128]{2,1,0:T(8,128)(2,1)S(1)}, bf16[1,4096,128]{2,1,0:T(8,128)(2,1)S(1)}, u32[]{:S(2)}, u32[]{:S(2)}) %collective-permute-start.29) | collective-permute-done | bytes 1048608 | tf_op jit(solution)/shard_map/ppermute | solution.py:278
  178.4 2.5 %collective-permute-done.31 = f32[2,64,128]{2,1,0:T(8,128)S(1)} collective-permute-done((f32[2,64,128]{2,1,0:T(8,128)S(1)}, f32[2,64,128]{2,1,0:T(8,128)S(1)}, u32[]{:S(2)}, u32[]{:S(2)}) %collective-permute-start.31) | collective-permute-done | bytes 65568 | tf_op jit(solution)/shard_map/ppermute | solution.py:278
  (132 shorter events, 49.3 us)
Async XLA Ops:
  5.6 6.0 %collective-permute-start = (bf16[8,64,128]{2,1,0:T(8,128)(2,1)S(1)}, bf16[8,64,128]{2,1,0:T(8,128)(2,1)S(1)}, u32[]{:S(2)}, u32[]{:S(2)}) collective-permute-start(bf16[8,64,128]{2,1,0:T(8,128)(2,1)S(1)} %get-tuple-element.54), channel_id=1, source_target_pairs={{0,16},{1,17},{2,18},{3,19},{4,20},{5,21},{6,22},{7,23},{8,24},{9,... | collective-permute-start | bytes 393224 | tf_op jit(solution)/shard_map/ppermute | solution.py:274
  9.2 6.0 %collective-permute-start.2 = (bf16[8,64,128]{2,1,0:T(8,128)(2,1)S(1)}, bf16[8,64,128]{2,1,0:T(8,128)(2,1)S(1)}, u32[]{:S(2)}, u32[]{:S(2)}) collective-permute-start(bf16[8,64,128]{2,1,0:T(8,128)(2,1)S(1)} %get-tuple-element.55), channel_id=1, source_target_pairs={{0,24},{1,25},{2,26},{3,27},{4,28},{5,29},{6,30},{7,31},{8,0},{9,1... | collective-permute-start | bytes 393224 | tf_op jit(solution)/shard_map/ppermute | solution.py:274
  10.1 7.4 %collective-permute-start.1 = (bf16[8,64,128]{2,1,0:T(8,128)(2,1)S(1)}, bf16[8,64,128]{2,1,0:T(8,128)(2,1)S(1)}, u32[]{:S(2)}, u32[]{:S(2)}) collective-permute-start(bf16[8,64,128]{2,1,0:T(8,128)(2,1)S(1)} %get-tuple-element.56), channel_id=1, source_target_pairs={{0,8},{1,9},{2,10},{3,11},{4,12},{5,13},{6,14},{7,15},{8,16},{9,17... | collective-permute-start | bytes 393224 | tf_op jit(solution)/shard_map/ppermute | solution.py:274
  43.3 6.9 %collective-permute-start.5 = (bf16[8,64,128]{2,1,0:T(8,128)(2,1)}, bf16[8,64,128]{2,1,0:T(8,128)(2,1)}, u32[]{:S(2)}, u32[]{:S(2)}) collective-permute-start(bf16[8,64,128]{2,1,0:T(8,128)(2,1)} %all_to_all.31.p0), channel_id=1, source_target_pairs={{0,24},{1,25},{2,26},{3,27},{4,28},{5,29},{6,30},{7,31},{8,0},{9,1... | collective-permute-start | bytes 393224 | tf_op jit(solution)/shard_map/ppermute | solution.py:274
  46.3 5.7 %collective-permute-start.4 = (bf16[8,64,128]{2,1,0:T(8,128)(2,1)}, bf16[8,64,128]{2,1,0:T(8,128)(2,1)}, u32[]{:S(2)}, u32[]{:S(2)}) collective-permute-start(bf16[8,64,128]{2,1,0:T(8,128)(2,1)} %all_to_all.31.p0), channel_id=1, source_target_pairs={{0,16},{1,17},{2,18},{3,19},{4,20},{5,21},{6,22},{7,23},{8,24},{9,... | collective-permute-start | bytes 393224 | tf_op jit(solution)/shard_map/ppermute | solution.py:274
  47.0 6.3 %collective-permute-start.3 = (bf16[8,64,128]{2,1,0:T(8,128)(2,1)}, bf16[8,64,128]{2,1,0:T(8,128)(2,1)}, u32[]{:S(2)}, u32[]{:S(2)}) collective-permute-start(bf16[8,64,128]{2,1,0:T(8,128)(2,1)} %all_to_all.31.p0), channel_id=1, source_target_pairs={{0,8},{1,9},{2,10},{3,11},{4,12},{5,13},{6,14},{7,15},{8,16},{9,17... | collective-permute-start | bytes 393224 | tf_op jit(solution)/shard_map/ppermute | solution.py:274
  59.4 6.7 %collective-permute-start.6 = (bf16[32,64,128]{2,1,0:T(8,128)(2,1)}, bf16[32,64,128]{2,1,0:T(8,128)(2,1)}, u32[]{:S(2)}, u32[]{:S(2)}) collective-permute-start(bf16[32,64,128]{2,1,0:T(8,128)(2,1)} %get-tuple-element.28), channel_id=1, source_target_pairs={{0,32},{32,0},{64,96},{96,64},{128,160},{160,128},{192,224},{224,1... | collective-permute-start | bytes 1572872 | tf_op jit(solution)/shard_map/ppermute | solution.py:278
  68.2 9.0 %collective-permute-start.7 = (bf16[8,64,128]{2,1,0:T(8,128)(2,1)S(1)}, bf16[8,64,128]{2,1,0:T(8,128)(2,1)S(1)}, u32[]{:S(2)}, u32[]{:S(2)}) collective-permute-start(bf16[8,64,128]{2,1,0:T(8,128)(2,1)S(1)} %get-tuple-element.30), channel_id=1, source_target_pairs={{0,16},{1,17},{2,18},{3,19},{4,20},{5,21},{6,22},{7,23},{8,24},{9,... | collective-permute-start | bytes 393224 | tf_op jit(solution)/shard_map/ppermute | solution.py:274
  69.0 9.0 %collective-permute-start.8 = (bf16[8,64,128]{2,1,0:T(8,128)(2,1)S(1)}, bf16[8,64,128]{2,1,0:T(8,128)(2,1)S(1)}, u32[]{:S(2)}, u32[]{:S(2)}) collective-permute-start(bf16[8,64,128]{2,1,0:T(8,128)(2,1)S(1)} %get-tuple-element.31), channel_id=1, source_target_pairs={{0,8},{1,9},{2,10},{3,11},{4,12},{5,13},{6,14},{7,15},{8,16},{9,17... | collective-permute-start | bytes 393224 | tf_op jit(solution)/shard_map/ppermute | solution.py:274
  69.2 8.9 %collective-permute-start.9 = (bf16[8,64,128]{2,1,0:T(8,128)(2,1)S(1)}, bf16[8,64,128]{2,1,0:T(8,128)(2,1)S(1)}, u32[]{:S(2)}, u32[]{:S(2)}) collective-permute-start(bf16[8,64,128]{2,1,0:T(8,128)(2,1)S(1)} %get-tuple-element.32), channel_id=1, source_target_pairs={{0,24},{1,25},{2,26},{3,27},{4,28},{5,29},{6,30},{7,31},{8,0},{9,1... | collective-permute-start | bytes 393224 | tf_op jit(solution)/shard_map/ppermute | solution.py:274
  73.0 30.0 %collective-permute-start.13 = (bf16[1,4096,128]{2,1,0:T(8,128)(2,1)S(1)}, bf16[1,4096,128]{2,1,0:T(8,128)(2,1)S(1)}, u32[]{:S(2)}, u32[]{:S(2)}) collective-permute-start(bf16[1,4096,128]{2,1,0:T(8,128)(2,1)S(1)} %constant_dynamic-slice_fusion.3), channel_id=1, source_target_pairs={{0,32},{32,0},{64,96},{96,64},{128,160},{160,128},{192,224},{224,1... | collective-permute-start | bytes 3145736 | tf_op jit(solution)/shard_map/ppermute | solution.py:278
  77.1 24.2 %collective-permute-start.17 = (bf16[64,64,128]{2,1,0:T(8,128)(2,1)S(1)}, bf16[64,64,128]{2,1,0:T(8,128)(2,1)S(1)}, u32[]{:S(2)}, u32[]{:S(2)}) collective-permute-start(bf16[64,64,128]{2,1,0:T(8,128)(2,1)S(1)} %get-tuple-element.37), channel_id=1, source_target_pairs={{0,32},{32,0},{64,96},{96,64},{128,160},{160,128},{192,224},{224,1... | collective-permute-start | bytes 3145736 | tf_op jit(solution)/shard_map/ppermute | solution.py:278
  100.5 6.0 %collective-permute-start.10 = (bf16[8,64,128]{2,1,0:T(8,128)(2,1)S(1)}, bf16[8,64,128]{2,1,0:T(8,128)(2,1)S(1)}, u32[]{:S(2)}, u32[]{:S(2)}) collective-permute-start(bf16[8,64,128]{2,1,0:T(8,128)(2,1)S(1)} %all_to_all.33.p0), channel_id=1, source_target_pairs={{0,8},{1,9},{2,10},{3,11},{4,12},{5,13},{6,14},{7,15},{8,16},{9,17... | collective-permute-start | bytes 393224 | tf_op jit(solution)/shard_map/ppermute | solution.py:274
  101.6 18.4 %collective-permute-start.18 = (bf16[32,64,128]{2,1,0:T(8,128)(2,1)S(1)}, bf16[32,64,128]{2,1,0:T(8,128)(2,1)S(1)}, u32[]{:S(2)}, u32[]{:S(2)}) collective-permute-start(bf16[32,64,128]{2,1,0:T(8,128)(2,1)S(1)} %get-tuple-element.39), channel_id=1, source_target_pairs={{0,64},{32,96},{64,0},{96,32},{128,192},{160,224},{192,128},{224,1... | collective-permute-start | bytes 1572872 | tf_op jit(solution)/shard_map/ppermute | solution.py:278
  107.6 6.7 %collective-permute-start.14 = (f32[64,128]{1,0:T(8,128)S(1)}, f32[64,128]{1,0:T(8,128)S(1)}, u32[]{:S(2)}, u32[]{:S(2)}) collective-permute-start(f32[64,128]{1,0:T(8,128)S(1)} %get-tuple-element.34), channel_id=1, source_target_pairs={{0,32},{32,0},{64,96},{96,64},{128,160},{160,128},{192,224},{224,1... | collective-permute-start | bytes 98312 | tf_op jit(solution)/shard_map/ppermute | solution.py:278
  120.9 9.3 %collective-permute-start.22 = (bf16[8,64,128]{2,1,0:T(8,128)(2,1)S(1)}, bf16[8,64,128]{2,1,0:T(8,128)(2,1)S(1)}, u32[]{:S(2)}, u32[]{:S(2)}) collective-permute-start(bf16[8,64,128]{2,1,0:T(8,128)(2,1)S(1)} %get-tuple-element.42), channel_id=1, source_target_pairs={{0,16},{1,17},{2,18},{3,19},{4,20},{5,21},{6,22},{7,23},{8,24},{9,... | collective-permute-start | bytes 393224 | tf_op jit(solution)/shard_map/ppermute | solution.py:274
  122.9 7.7 %collective-permute-start.23 = (bf16[8,64,128]{2,1,0:T(8,128)(2,1)S(1)}, bf16[8,64,128]{2,1,0:T(8,128)(2,1)S(1)}, u32[]{:S(2)}, u32[]{:S(2)}) collective-permute-start(bf16[8,64,128]{2,1,0:T(8,128)(2,1)S(1)} %get-tuple-element.43), channel_id=1, source_target_pairs={{0,8},{1,9},{2,10},{3,11},{4,12},{5,13},{6,14},{7,15},{8,16},{9,17... | collective-permute-start | bytes 393224 | tf_op jit(solution)/shard_map/ppermute | solution.py:274
  122.9 7.7 %collective-permute-start.24 = (bf16[8,64,128]{2,1,0:T(8,128)(2,1)S(1)}, bf16[8,64,128]{2,1,0:T(8,128)(2,1)S(1)}, u32[]{:S(2)}, u32[]{:S(2)}) collective-permute-start(bf16[8,64,128]{2,1,0:T(8,128)(2,1)S(1)} %get-tuple-element.44), channel_id=1, source_target_pairs={{0,24},{1,25},{2,26},{3,27},{4,28},{5,29},{6,30},{7,31},{8,0},{9,1... | collective-permute-start | bytes 393224 | tf_op jit(solution)/shard_map/ppermute | solution.py:274
  127.6 26.5 %collective-permute-start.30 = (bf16[1,4096,128]{2,1,0:T(8,128)(2,1)S(1)}, bf16[1,4096,128]{2,1,0:T(8,128)(2,1)S(1)}, u32[]{:S(2)}, u32[]{:S(2)}) collective-permute-start(bf16[1,4096,128]{2,1,0:T(8,128)(2,1)S(1)} %get-tuple-element.51), channel_id=1, source_target_pairs={{0,96},{32,64},{64,32},{96,0},{128,224},{160,192},{192,160},{224,1... | collective-permute-start | bytes 3145736 | tf_op jit(solution)/shard_map/ppermute | solution.py:278
  130.1 46.3 %collective-permute-start.29 = (bf16[1,4096,128]{2,1,0:T(8,128)(2,1)S(1)}, bf16[1,4096,128]{2,1,0:T(8,128)(2,1)S(1)}, u32[]{:S(2)}, u32[]{:S(2)}) collective-permute-start(bf16[1,4096,128]{2,1,0:T(8,128)(2,1)S(1)} %get-tuple-element.52), channel_id=1, source_target_pairs={{0,64},{32,96},{64,0},{96,32},{128,192},{160,224},{192,128},{224,1... | collective-permute-start | bytes 3145736 | tf_op jit(solution)/shard_map/ppermute | solution.py:278
  130.3 46.1 %collective-permute-start.28 = (bf16[1,4096,128]{2,1,0:T(8,128)(2,1)S(1)}, bf16[1,4096,128]{2,1,0:T(8,128)(2,1)S(1)}, u32[]{:S(2)}, u32[]{:S(2)}) collective-permute-start(bf16[1,4096,128]{2,1,0:T(8,128)(2,1)S(1)} %get-tuple-element.53), channel_id=1, source_target_pairs={{0,32},{32,0},{64,96},{96,64},{128,160},{160,128},{192,224},{224,1... | collective-permute-start | bytes 3145736 | tf_op jit(solution)/shard_map/ppermute | solution.py:278
  152.1 24.3 %collective-permute-start.27 = (bf16[8,64,128]{2,1,0:T(8,128)(2,1)S(1)}, bf16[8,64,128]{2,1,0:T(8,128)(2,1)S(1)}, u32[]{:S(2)}, u32[]{:S(2)}) collective-permute-start(bf16[8,64,128]{2,1,0:T(8,128)(2,1)S(1)} %all_to_all.35.p0), channel_id=1, source_target_pairs={{0,24},{1,25},{2,26},{3,27},{4,28},{5,29},{6,30},{7,31},{8,0},{9,1... | collective-permute-start | bytes 393224 | tf_op jit(solution)/shard_map/ppermute | solution.py:274
  152.7 23.6 %collective-permute-start.26 = (bf16[8,64,128]{2,1,0:T(8,128)(2,1)S(1)}, bf16[8,64,128]{2,1,0:T(8,128)(2,1)S(1)}, u32[]{:S(2)}, u32[]{:S(2)}) collective-permute-start(bf16[8,64,128]{2,1,0:T(8,128)(2,1)S(1)} %all_to_all.35.p0), channel_id=1, source_target_pairs={{0,16},{1,17},{2,18},{3,19},{4,20},{5,21},{6,22},{7,23},{8,24},{9,... | collective-permute-start | bytes 393224 | tf_op jit(solution)/shard_map/ppermute | solution.py:274
  154.1 22.3 %collective-permute-start.25 = (bf16[8,64,128]{2,1,0:T(8,128)(2,1)S(1)}, bf16[8,64,128]{2,1,0:T(8,128)(2,1)S(1)}, u32[]{:S(2)}, u32[]{:S(2)}) collective-permute-start(bf16[8,64,128]{2,1,0:T(8,128)(2,1)S(1)} %all_to_all.35.p0), channel_id=1, source_target_pairs={{0,8},{1,9},{2,10},{3,11},{4,12},{5,13},{6,14},{7,15},{8,16},{9,17... | collective-permute-start | bytes 393224 | tf_op jit(solution)/shard_map/ppermute | solution.py:274
  (31 other events, 419.6 us)

commit v2 on v1

v2 whole, which is shorter than its diff:
```python
import functools

import jax
import jax.numpy as jnp
from jax import lax
from jax.experimental import pallas as pl
from jax.experimental.pallas import tpu as pltpu
from jax.sharding import PartitionSpec as P

ALONG_X = 4
DEPTH = 8
BF16 = jnp.bfloat16
F32 = jnp.float32
WHOLE = pl.BlockSpec(memory_space=pltpu.VMEM)
SCALARS = pl.BlockSpec(memory_space=pltpu.SMEM)
PARAMS = pltpu.CompilerParams(vmem_limit_bytes=20 * 2**20)


def here():
    group = lax.axis_index("group").astype(jnp.int32)
    x = lax.div(lax.axis_index("member").astype(jnp.int32), DEPTH)
    return x, group & 1, lax.shift_right_logical(group, 1) & 1, group & 3


def slot(entry, place):
    x = place[0]
    z = lax.rem(entry, DEPTH)
    step = (lax.div(entry, DEPTH) + (ALONG_X - x)) & (ALONG_X - 1)
    return lax.rem(step, ALONG_X) * DEPTH + z


def slot_at(entry, place, level):
    members = ALONG_X * DEPTH
    inner = slot(lax.rem(entry, members), place)
    group = lax.div(entry, members)
    core = (group & 1) ^ place[1]
    if level == 0:
        return inner
    if level == 1:
        return core * members + inner
    high = (lax.div(group, 2) & 1) ^ place[2]
    return core * (2 * members) + high * members + inner


def leaf_kernel(level, each, rows, values, panels, *refs):
    outs, total = refs[:-1], refs[-1]
    blocks = total.shape[0]
    step = pl.program_id(0)
    place = here()

    @pl.when(step == 0)
    def _():
        @pl.loop(0, blocks // 8)
        def _(i):
            total[pl.ds(i * 8, 8)] = jnp.zeros((8, *total.shape[1:]), F32)

    for k in range(each):
        value = values[k]
        for t in range(panels.shape[2]):
            at = slot_at(rows[level, t, step * each + k], place, level)
            total[at] += jnp.dot(value, panels[k, 0, t], preferred_element_type=F32)

    @pl.when(step == pl.num_programs(0) - 1)
    def _():
        held = blocks // len(outs)
        for k, out in enumerate(outs):

            @pl.loop(0, held // 8)
            def _(i):
                out[pl.ds(i * 8, 8)] = total[pl.ds(k * held + i * 8, 8)].astype(BF16)


def leaf_sums(level, rows, values, panels):
    count, _, targets, p, q = panels.shape
    height = values.shape[1]
    blocks = ALONG_X * DEPTH * 2**level
    each = count // 2 if level == 0 else count
    outs = ALONG_X if level == 0 else 1
    return pl.pallas_call(
        functools.partial(leaf_kernel, level, each),
        grid=(count // each,),
        in_specs=[
            SCALARS,
            pl.BlockSpec((each, height, p), lambda i: (i, 0, 0)),
            pl.BlockSpec((each, 1, targets, p, q), lambda i: (i, level, 0, 0, 0)),
        ],
        out_specs=[pl.BlockSpec((blocks // outs, height, q), lambda i: (0, 0, 0))] * outs,
        out_shape=[jax.ShapeDtypeStruct((blocks // outs, height, q), BF16)] * outs,
        scratch_shapes=[pltpu.VMEM((blocks, height, q), F32)],
        compiler_params=pltpu.CompilerParams(vmem_limit_bytes=61 * 2**20)
        if level == 0
        else PARAMS,
        cost_estimate=pl.CostEstimate(
            flops=2 * count * targets * height * p * q,
            bytes_accessed=2 * count * targets * p * q + 2 * blocks * height * q,
            transcendentals=0,
        ),
    )(rows, values, panels)


def partial_kernel(sets, p0, p1, p2, p3, *refs):
    weights, outs = refs[:sets], refs[sets:]
    place = here()
    first = (0, place[1], 0, place[3])[sets - 1] * (ALONG_X * DEPTH * 128)
    sums = [None] * sets
    depth = DEPTH * 128
    for k, part in enumerate((p0, p1, p2, p3)):
        lhs = jnp.concatenate([part[z] for z in range(DEPTH)], axis=1)
        start = pl.multiple_of(((place[0] + ALONG_X - k) & (ALONG_X - 1)) * depth, depth)
        for s in range(sets):
            at = pl.multiple_of(start + first, depth) if s == 0 else start
            term = jnp.dot(lhs, weights[s][0, pl.ds(at, depth), :], preferred_element_type=F32)
            sums[s] = term if sums[s] is None else sums[s] + term
    for s in range(sets):
        outs[s][...] = sums[s].astype(outs[s].dtype)


def partials(parts, inverse, others, kind):
    rows, columns = ALONG_X * DEPTH * 128, inverse.shape[-1]
    height = parts[0].shape[1]
    sets = 1 + len(others)
    return pl.pallas_call(
        functools.partial(partial_kernel, sets),
        in_specs=[WHOLE] * (4 + sets),
        out_specs=[WHOLE] * sets,
        out_shape=[jax.ShapeDtypeStruct((height, columns), kind)] * sets,
        compiler_params=PARAMS,
        cost_estimate=pl.CostEstimate(
            flops=2 * sets * height * rows * columns,
            bytes_accessed=2 * sets * rows * columns,
            transcendentals=0,
        ),
    )(*parts, inverse, *others)


def add_kernel(level, pair, rows, value, panels, base, keep, send):
    half = keep.shape[0]
    place = here()

    @pl.loop(0, half // 8)
    def _(i):
        keep[pl.ds(i * 8, 8)] = base[pl.ds(i * 8, 8)]
        send[pl.ds(i * 8, 8)] = base[pl.ds(half + i * 8, 8)]

    lhs = value[...]
    for t in range(panels.shape[2]):
        at = slot_at(rows[pair, 0, t], place, level)
        term = jnp.dot(lhs, panels[0, 0, t], preferred_element_type=F32)

        @pl.when(at < half)
        def _():
            keep[at] = (keep[at].astype(F32) + term).astype(BF16)

        @pl.when(at >= half)
        def _():
            send[at - half] = (send[at - half].astype(F32) + term).astype(BF16)


def add_terms(level, pair, rows, value, panels, base):
    blocks, height, columns = base.shape
    targets, p = panels.shape[2:4]
    half = jax.ShapeDtypeStruct((blocks // 2, height, columns), BF16)
    fixed = lambda *dims: pl.BlockSpec(dims, lambda i: (0,) * len(dims))
    return pl.pallas_call(
        functools.partial(add_kernel, level, pair),
        grid=(1,),
        in_specs=[
            SCALARS,
            fixed(height, p),
            pl.BlockSpec((1, 1, targets, p, columns), lambda i: (0, pair, 0, 0, 0)),
            fixed(*base.shape),
        ],
        out_specs=[fixed(*half.shape)] * 2,
        out_shape=[half, half],
        compiler_params=PARAMS,
        cost_estimate=pl.CostEstimate(
            flops=2 * targets * height * p * columns,
            bytes_accessed=4 * blocks * height * columns,
            transcendentals=0,
        ),
    )(rows, value, panels, base)


def pieces_kernel(parts, a, b, *outs):
    each = a.shape[0] // parts

    for k in range(parts):

        @pl.loop(0, each // 8)
        def _(i):
            at = pl.ds(k * each + i * 8, 8)
            outs[k][pl.ds(i * 8, 8)] = (a[at].astype(F32) + b[at].astype(F32)).astype(BF16)


def sum_in_pieces(a, b, parts):
    piece = jax.ShapeDtypeStruct((a.shape[0] // parts, *a.shape[1:]), BF16)
    return pl.pallas_call(
        functools.partial(pieces_kernel, parts),
        in_specs=[WHOLE] * 2,
        out_specs=[WHOLE] * parts,
        out_shape=[piece] * parts,
        compiler_params=PARAMS,
        cost_estimate=pl.CostEstimate(flops=a.size, bytes_accessed=6 * a.size, transcendentals=0),
    )(a, b)


def terms_kernel(mine, other, panels, out, solution):
    solved = (mine[...] + other[...]).astype(BF16)
    solution[...] = solved
    for t in range(panels.shape[2]):
        out[t] = jnp.dot(solved, panels[0, 0, t], preferred_element_type=F32).astype(BF16)


def solve_and_terms(mine, other, panels, pair):
    height, columns = mine.shape
    targets, p = panels.shape[2:4]
    fixed = lambda *dims: pl.BlockSpec(dims, lambda i: (0,) * len(dims))
    return pl.pallas_call(
        terms_kernel,
        grid=(1,),
        in_specs=[
            fixed(height, columns),
            fixed(height, columns),
            pl.BlockSpec((1, 1, targets, p, columns), lambda i: (0, pair, 0, 0, 0)),
        ],
        out_specs=[fixed(targets, height, columns), fixed(height, columns)],
        out_shape=[
            jax.ShapeDtypeStruct((targets, height, columns), BF16),
            jax.ShapeDtypeStruct((height, columns), BF16),
        ],
        compiler_params=PARAMS,
        cost_estimate=pl.CostEstimate(
            flops=2 * targets * height * p * columns,
            bytes_accessed=4 * targets * p * columns,
            transcendentals=0,
        ),
        name="terms",
    )(mine, other, panels)


def merge_kernel(rows, a, b, *refs):
    place = here()
    terms, outs, total = refs[:4], refs[4:8], refs[8]
    blocks = a.shape[0]
    members = ALONG_X * DEPTH

    @pl.loop(0, blocks // 8)
    def _(i):
        at = pl.ds(i * 8, 8)
        total[at] = a[at].astype(F32) + b[at].astype(F32)

    for source, term in enumerate(terms):
        for t in range(term.shape[0]):
            entry = rows[source, t]

            @pl.when(lax.div(entry, members) == place[3])
            def _():
                at = slot(lax.rem(entry, members), place)
                total[at] += term[t].astype(F32)

    for k in range(ALONG_X):
        outs[k][...] = total[pl.ds(k * DEPTH, DEPTH)].astype(BF16)


def merge(rows, a, b, terms):
    piece = jax.ShapeDtypeStruct((DEPTH, *a.shape[1:]), BF16)
    return pl.pallas_call(
        merge_kernel,
        in_specs=[SCALARS] + [WHOLE] * 6,
        out_specs=[WHOLE] * ALONG_X,
        out_shape=[piece] * ALONG_X,
        scratch_shapes=[pltpu.VMEM(a.shape, F32)],
        compiler_params=PARAMS,
        cost_estimate=pl.CostEstimate(flops=a.size, bytes_accessed=6 * a.size, transcendentals=0),
        name="merge",
    )(rows, a, b, *terms)


def along_x(value, step):
    pairs = [
        (x * DEPTH + z, (x + step) % ALONG_X * DEPTH + z)
        for x in range(ALONG_X)
        for z in range(DEPTH)
    ]
    return lax.ppermute(value, "member", pairs)


def swapped(value, mask):
    return lax.ppermute(value, "group", [(g, g ^ mask) for g in range(lax.axis_size("group"))])


def over_z(pieces):
    groups = [[x * DEPTH + z for z in range(DEPTH)] for x in range(ALONG_X)]
    return lax.all_to_all(pieces, "member", 0, 0, axis_index_groups=groups, tiled=True)


def resid_kernel(level, arrived, right, out):
    total = right[level, 0].astype(F32)
    for z in range(DEPTH):
        total = total - arrived[z].astype(F32)
    resid = total.astype(BF16)
    for z in range(DEPTH):
        out[z] = resid


def residual_copies(arrived, right, level):
    return pl.pallas_call(
        functools.partial(resid_kernel, level),
        in_specs=[WHOLE] * 2,
        out_specs=WHOLE,
        out_shape=jax.ShapeDtypeStruct(arrived.shape, BF16),
        compiler_params=PARAMS,
        cost_estimate=pl.CostEstimate(flops=arrived.size, bytes_accessed=4 * arrived.size, transcendentals=0),
    )(arrived, right)


def collect(pieces, right, level):
    arrived = [along_x(pieces[k], k) for k in (2, 1, 3)]
    total = pieces[0].astype(F32)
    for part in arrived:
        total = total + part.astype(F32)
    total = total.astype(BF16)
    return residual_copies(over_z(total), right, level)


def gather(copies):
    own = over_z(copies)
    far = along_x(own, 2)
    near = [along_x(own, k) for k in (1, 3)]
    return own, near[0], far, near[1]


def on_device(
    leaf_solution,
    leaf_panels,
    leaf_rows,
    sep_panels,
    sep_rows,
    right_sides,
    inverse_low,
    inverse_mid,
    inverse_top,
):
    quarter = lax.axis_index("group").astype(jnp.int32) & 3
    rows = leaf_rows.transpose(1, 2, 0)
    source = sep_rows.transpose(1, 0, 2)
    span = ALONG_X * DEPTH * inverse_low.shape[-1]

    def turned(inverse, at):
        return lax.dynamic_slice_in_dim(inverse, at * span, span, 1)

    pieces = leaf_sums(0, rows, leaf_solution, leaf_panels)

    mid_other = swapped(turned(inverse_mid, quarter & 1 ^ 1), 1)
    top_others = []
    for mask in (1, 2, 3):
        top_others.append(swapped(turned(inverse_top, quarter ^ mask), mask))
    rows_mine = source[2]
    rows_high = swapped(rows_mine, 2)
    rows_two = jnp.concatenate([rows_mine, rows_high])
    rows_core = swapped(rows_two, 1)
    rows_all = jnp.concatenate([rows_two, rows_core])

    (base_mid,) = leaf_sums(1, rows, leaf_solution, leaf_panels)
    (base_top,) = leaf_sums(2, rows, leaf_solution, leaf_panels)

    copies = collect(pieces, right_sides, 0)
    (first,) = partials(gather(copies), inverse_low, [], BF16)

    keep, send = add_terms(1, 0, source, first, sep_panels, base_mid)
    copies = collect(sum_in_pieces(keep, swapped(send, 1), ALONG_X), right_sides, 1)

    keep_top, send_top = add_terms(2, 1, source, first, sep_panels, base_top)
    stay, leave = sum_in_pieces(keep_top, swapped(send_top, 1), 2)
    arrived = swapped(leave, 2)

    mine, theirs = partials(gather(copies), inverse_mid, [mid_other], F32)
    terms, second = solve_and_terms(mine, swapped(theirs, 1), sep_panels, 2)
    terms_high = swapped(terms, 2)
    terms_core = swapped(terms, 1)
    terms_both = swapped(terms_high, 1)
    pieces = merge(rows_all, stay, arrived, [terms, terms_high, terms_core, terms_both])
    copies = collect(pieces, right_sides, 2)
    mine, by_core, by_high, by_both = partials(gather(copies), inverse_top, top_others, F32)
    pair = swapped(jnp.stack([by_high, by_both]), 2)
    third = (mine + pair[0] + swapped(by_core + pair[1], 1)).astype(BF16)
    return jnp.stack([first, second, third])[:, None]


def solution(mesh):
    placed = (
        P(("group", "member"), None, None),
        P(("group", "member"), None, None, None, None),
        P(("group", "member"), None, None),
        P(("group", "member"), None, None, None, None),
        P(("group", "member"), None, None),
        P(None, ("group", "member"), None, None),
        P(("group", "member"), None, None),
        P(("group", "member"), None, None),
        P(("group", "member"), None, None),
    )
    return jax.shard_map(
        on_device,
        mesh=mesh,
        in_specs=placed,
        out_specs=P(None, ("group", "member"), None, None),
        check_vma=False,
    )
```

time: 185 us -> 200 us (1.081)
  waiting for transfers between devices: 44.6 us -> 58.3 us
  starting transfers between devices: 42.4 us -> 55.3 us
  blocking collectives: 66.5 us -> 57.3 us
  local copies, waits for them, and re-layouts: 12.4 us -> 9.02 us
  Pallas kernels: 13.9 us -> 16.9 us
  other arithmetic: 4.01 us -> 1.8 us
    all_to_all x6 -> x5, blocking collectives: 66.5 us -> 57.3 us  [over_z(): lax.all_to_all(pieces, 'member', 0, 0, axis_index_groups=groups, tiled=True)]
    ppermute x18, waiting for transfers between devices: 14.2 us -> 22.2 us  [along_x(): return lax.ppermute(value, 'member', pairs)]
    all_to_all x0 -> x1, waiting for transfers between devices: none -> 7.9 us  [over_z(): lax.all_to_all(pieces, 'member', 0, 0, axis_index_groups=groups, tiled=True)]
    ppermute x15, starting transfers between devices: 21.8 us -> 28.8 us  [swapped(): lax.ppermute(value, 'group', [(g, g ^ mask) for g in range(lax.axis_size(...]
    all_to_all x0 -> x1, starting transfers between devices: none -> 4 us  [over_z(): lax.all_to_all(pieces, 'member', 0, 0, axis_index_groups=groups, tiled=True)]
    ppermute x15, waiting for transfers between devices: 30.4 us -> 28.3 us  [swapped(): lax.ppermute(value, 'group', [(g, g ^ mask) for g in range(lax.axis_size(...]
    dynamic_slice x2, local copies, waits for them, and re-layouts: 3.35 us -> 1.24 us  [turned(): return lax.dynamic_slice_in_dim(inverse, at * span, span, 1)]
    unnamed x45 -> x42, local copies, waits for them, and re-layouts: 7.63 us -> 7.13 us
  transfers between devices with their start and end apart: 33 -> 34, of which waited for: 17 -> 17; matrix products, arithmetic and copies ran while one was open for 4% -> 1% of each run, Pallas kernels for 3% -> 6%
where the time goes in v2:
time: 200 us; the launch traced here: 199 us
  waiting for transfers between devices  58.3 us (29%)
  blocking collectives  57.3 us (29%)
  starting transfers between devices  55.3 us (28%)
  Pallas kernels  16.9 us (8%)
  local copies, waits for them, and re-layouts  9.02 us (5%)
    all_to_all x5, blocking collectives, over_z(): lax.all_to_all(pieces, 'member', 0, 0, axis_index_groups=groups, tiled=True)  57.3 us
    ppermute x15, starting transfers between devices, swapped(): lax.ppermute(value, 'group', [(g, g ^ mask) for g in range(lax.axis_size(...  28.8 us
    ppermute x15, waiting for transfers between devices, swapped(): lax.ppermute(value, 'group', [(g, g ^ mask) for g in range(lax.axis_size(...  28.3 us
    ppermute x18, starting transfers between devices, along_x(): return lax.ppermute(value, 'member', pairs)  22.4 us
    ppermute x18, waiting for transfers between devices, along_x(): return lax.ppermute(value, 'member', pairs)  22.2 us
    all_to_all x1, waiting for transfers between devices, over_z(): lax.all_to_all(pieces, 'member', 0, 0, axis_index_groups=groups, tiled=True)  7.9 us
    unnamed x42, local copies, waits for them, and re-layouts  7.13 us
    pallas_call x3, Pallas kernels, leaf_sums(): pl.pallas_call(functools.partial(leaf_kernel, level, each), grid=(count /...  5.82 us
  transfers between devices with their start and end apart: 34, of which 17 were waited for; matrix products, arithmetic and copies ran while one was open for 1% of the time, Pallas kernels for 6%

profile of v2, /device:TPU:1, one launch (start us, length us, event | category | flops | bytes accessed | tf_op | source)
XLA Modules:
  0.0 198.9 jit_solution(368446233653479582)
XLA Ops:
  0.0 2.7 %shard_map.91 = (bf16[8,64,128]{2,1,0:T(8,128)(2,1)}, bf16[8,64,128]{2,1,0:T(8,128)(2,1)}, bf16[8,64,128]{2,1,0:T(8,128)(2,1)}, bf16[8,64,128]{2,1,0:T(8,128)(2,1)}) custom-call(s32[3,4,8]{2,1,0:T(4,128)} %bitcast.29, bf16[8,64,128]{2,1,0:T(8,128)(2,1)} %values.5, bf16[8,3,4,128,128]{4,3,2,1,0:T(8,128)(2,1)} %panels.10), custom_call_target="tpu_custom_call" | custom-call | flops 67108864 | bytes 1572864 | tf_op jit(solution)/shard_map/pallas_call | solution.py:79
  2.7 3.6 %collective-permute-start = (bf16[8,64,128]{2,1,0:T(8,128)(2,1)}, bf16[8,64,128]{2,1,0:T(8,128)(2,1)S(1)}, u32[]{:S(2)}, u32[]{:S(2)}) collective-permute-start(bf16[8,64,128]{2,1,0:T(8,128)(2,1)} %get-tuple-element.32), channel_id=1, source_target_pairs={{0,16},{1,17},{2,18},{3,19},{4,20},{5,21},{6,22},{7,23},{8,24},{9,... | collective-permute-start | bytes 393224 | tf_op jit(solution)/shard_map/ppermute | solution.py:285
  6.6 2.4 %collective-permute-start.2 = (bf16[8,64,128]{2,1,0:T(8,128)(2,1)}, bf16[8,64,128]{2,1,0:T(8,128)(2,1)S(1)}, u32[]{:S(2)}, u32[]{:S(2)}) collective-permute-start(bf16[8,64,128]{2,1,0:T(8,128)(2,1)} %get-tuple-element.34), channel_id=1, source_target_pairs={{0,24},{1,25},{2,26},{3,27},{4,28},{5,29},{6,30},{7,31},{8,0},{9,1... | collective-permute-start | bytes 393224 | tf_op jit(solution)/shard_map/ppermute | solution.py:285
  9.0 4.8 %collective-permute-done.1 = bf16[8,64,128]{2,1,0:T(8,128)(2,1)S(1)} collective-permute-done((bf16[8,64,128]{2,1,0:T(8,128)(2,1)}, bf16[8,64,128]{2,1,0:T(8,128)(2,1)S(1)}, u32[]{:S(2)}, u32[]{:S(2)}) %collective-permute-start.1) | collective-permute-done | bytes 131104 | tf_op jit(solution)/shard_map/ppermute | solution.py:285
  14.8 15.4 %all_to_all.30.arrived = bf16[8,64,128]{2,1,0:T(8,128)(2,1)S(1)} all-to-all(bf16[8,64,128]{2,1,0:T(8,128)(2,1)S(1)} %add_convert_fusion.2), channel_id=1, replica_groups={{0,1,2,3,4,5,6,7},{8,9,10,11,12,13,14,15},{16,17,18,19,20,21,22,23},{24..., dimensions={0} | all-to-all | bytes 262144 | tf_op jit(solution)/shard_map/all_to_all | solution.py:294
  30.2 10.5 %all_to_all.31.p0 = bf16[8,64,128]{2,1,0:T(8,128)(2,1)S(1)} all-to-all(bf16[8,64,128]{2,1,0:T(8,128)(2,1)S(1)} %shard_map.92), channel_id=1, replica_groups={{0,1,2,3,4,5,6,7},{8,9,10,11,12,13,14,15},{16,17,18,19,20,21,22,23},{24..., dimensions={0} | all-to-all | bytes 262144 | tf_op jit(solution)/shard_map/all_to_all | solution.py:294
  52.8 5.4 %collective-permute-start.6 = (bf16[32,64,128]{2,1,0:T(8,128)(2,1)}, bf16[32,64,128]{2,1,0:T(8,128)(2,1)}, u32[]{:S(2)}, u32[]{:S(2)}) collective-permute-start(bf16[32,64,128]{2,1,0:T(8,128)(2,1)} %get-tuple-element.36), channel_id=1, source_target_pairs={{0,32},{32,0},{64,96},{96,64},{128,160},{160,128},{192,224},{224,1... | collective-permute-start | bytes 1572872 | tf_op jit(solution)/shard_map/ppermute | solution.py:289
  61.6 2.3 %shard_map.100 = (bf16[64,64,128]{2,1,0:T(8,128)(2,1)S(1)}, bf16[64,64,128]{2,1,0:T(8,128)(2,1)}) custom-call(s32[3,1,4]{2,1,0:T(1,128)S(1)} %bitcast.36, bf16[64,128]{1,0:T(8,128)(2,1)S(1)} %shard_map.93.value, bf16[1,3,4,128,128]{4,3,2,1,0:T(8,128)(2,1)S(1)} %copy-done.5, bf16[128,64,128]{2,1,0:T(8,128)(2,1)S(1)} %shard_map.99.base), custom_call_target="tpu_custom_call" | custom-call | flops 8388608 | bytes 4194304 | tf_op jit(solution)/shard_map/pallas_call | solution.py:164
  72.0 3.4 %collective-permute-done.8 = bf16[8,64,128]{2,1,0:T(8,128)(2,1)S(1)} collective-permute-done((bf16[8,64,128]{2,1,0:T(8,128)(2,1)S(1)}, bf16[8,64,128]{2,1,0:T(8,128)(2,1)S(1)}, u32[]{:S(2)}, u32[]{:S(2)}) %collective-permute-start.8) | collective-permute-done | bytes 131104 | tf_op jit(solution)/shard_map/ppermute | solution.py:285
  75.4 10.6 %all_to_all.32.arrived = bf16[8,64,128]{2,1,0:T(8,128)(2,1)S(1)} all-to-all(bf16[8,64,128]{2,1,0:T(8,128)(2,1)S(1)} %add_convert_fusion.1), channel_id=1, replica_groups={{0,1,2,3,4,5,6,7},{8,9,10,11,12,13,14,15},{16,17,18,19,20,21,22,23},{24..., dimensions={0} | all-to-all | bytes 262144 | tf_op jit(solution)/shard_map/all_to_all | solution.py:294
  86.7 4.0 %all-to-all-start.3 = ((bf16[8,64,128]{2,1,0:T(8,128)(2,1)}), bf16[8,64,128]{2,1,0:T(8,128)(2,1)}, u32[]{:S(2)}, u32[]{:S(2)}) async-start(bf16[8,64,128]{2,1,0:T(8,128)(2,1)} %copy-done.13), calls=%async_computation.3 | async-start | bytes 262144 | tf_op jit(solution)/shard_map/all_to_all | solution.py:294
  90.7 7.9 %all-to-all-done.3.p0 = bf16[8,64,128]{2,1,0:T(8,128)(2,1)} async-done(((bf16[8,64,128]{2,1,0:T(8,128)(2,1)}), bf16[8,64,128]{2,1,0:T(8,128)(2,1)}, u32[]{:S(2)}, u32[]{:S(2)}) %all-to-all-start.3) | async-done | bytes 131104 | tf_op jit(solution)/shard_map/all_to_all | solution.py:294
  107.0 4.5 %collective-permute-start.14 = (f32[64,128]{1,0:T(8,128)S(1)}, f32[64,128]{1,0:T(8,128)S(1)}, u32[]{:S(2)}, u32[]{:S(2)}) collective-permute-start(f32[64,128]{1,0:T(8,128)S(1)} %get-tuple-element.42), channel_id=1, source_target_pairs={{0,32},{32,0},{64,96},{96,64},{128,160},{160,128},{192,224},{224,1... | collective-permute-start | bytes 98312 | tf_op jit(solution)/shard_map/ppermute | solution.py:289
  114.7 23.4 %collective-permute-done.19.refs_1_ = bf16[4,64,128]{2,1,0:T(8,128)(2,1)S(1)} collective-permute-done((bf16[4,64,128]{2,1,0:T(8,128)(2,1)S(1)}, bf16[4,64,128]{2,1,0:T(8,128)(2,1)S(1)}, u32[]{:S(2)}, u32[]{:S(2)}) %collective-permute-start.19) | collective-permute-done | bytes 65568 | tf_op jit(solution)/shard_map/ppermute | solution.py:289
  138.1 5.0 %collective-permute-start.21 = (bf16[4,64,128]{2,1,0:T(8,128)(2,1)S(1)}, bf16[4,64,128]{2,1,0:T(8,128)(2,1)S(1)}, u32[]{:S(2)}, u32[]{:S(2)}) collective-permute-start(bf16[4,64,128]{2,1,0:T(8,128)(2,1)S(1)} %collective-permute-done.19.refs_1_), channel_id=1, source_target_pairs={{0,32},{32,0},{64,96},{96,64},{128,160},{160,128},{192,224},{224,1... | collective-permute-start | bytes 196616 | tf_op jit(solution)/shard_map/ppermute | solution.py:289
  145.0 3.7 %collective-permute-start.22 = (bf16[8,64,128]{2,1,0:T(8,128)(2,1)S(1)}, bf16[8,64,128]{2,1,0:T(8,128)(2,1)S(1)}, u32[]{:S(2)}, u32[]{:S(2)}) collective-permute-start(bf16[8,64,128]{2,1,0:T(8,128)(2,1)S(1)} %get-tuple-element.50), channel_id=1, source_target_pairs={{0,16},{1,17},{2,18},{3,19},{4,20},{5,21},{6,22},{7,23},{8,24},{9,... | collective-permute-start | bytes 393224 | tf_op jit(solution)/shard_map/ppermute | solution.py:285
  149.7 2.4 %collective-permute-done.22 = bf16[8,64,128]{2,1,0:T(8,128)(2,1)S(1)} collective-permute-done((bf16[8,64,128]{2,1,0:T(8,128)(2,1)S(1)}, bf16[8,64,128]{2,1,0:T(8,128)(2,1)S(1)}, u32[]{:S(2)}, u32[]{:S(2)}) %collective-permute-start.22) | collective-permute-done | bytes 131104 | tf_op jit(solution)/shard_map/ppermute | solution.py:285
  153.6 2.3 %collective-permute-done.23 = bf16[8,64,128]{2,1,0:T(8,128)(2,1)S(1)} collective-permute-done((bf16[8,64,128]{2,1,0:T(8,128)(2,1)S(1)}, bf16[8,64,128]{2,1,0:T(8,128)(2,1)S(1)}, u32[]{:S(2)}, u32[]{:S(2)}) %collective-permute-start.23) | collective-permute-done | bytes 131104 | tf_op jit(solution)/shard_map/ppermute | solution.py:285
  156.3 10.4 %all_to_all.33.arrived = bf16[8,64,128]{2,1,0:T(8,128)(2,1)S(1)} all-to-all(bf16[8,64,128]{2,1,0:T(8,128)(2,1)S(1)} %add_convert_fusion), channel_id=1, replica_groups={{0,1,2,3,4,5,6,7},{8,9,10,11,12,13,14,15},{16,17,18,19,20,21,22,23},{24..., dimensions={0} | all-to-all | bytes 262144 | tf_op jit(solution)/shard_map/all_to_all | solution.py:294
  166.8 10.4 %all_to_all.34.p0 = bf16[8,64,128]{2,1,0:T(8,128)(2,1)S(1)} all-to-all(bf16[8,64,128]{2,1,0:T(8,128)(2,1)S(1)} %shard_map.102), channel_id=1, replica_groups={{0,1,2,3,4,5,6,7},{8,9,10,11,12,13,14,15},{16,17,18,19,20,21,22,23},{24..., dimensions={0} | all-to-all | bytes 262144 | tf_op jit(solution)/shard_map/all_to_all | solution.py:294
  177.2 2.4 %collective-permute-start.27 = (bf16[8,64,128]{2,1,0:T(8,128)(2,1)S(1)}, bf16[8,64,128]{2,1,0:T(8,128)(2,1)S(1)}, u32[]{:S(2)}, u32[]{:S(2)}) collective-permute-start(bf16[8,64,128]{2,1,0:T(8,128)(2,1)S(1)} %all_to_all.34.p0), channel_id=1, source_target_pairs={{0,24},{1,25},{2,26},{3,27},{4,28},{5,29},{6,30},{7,31},{8,0},{9,1... | collective-permute-start | bytes 393224 | tf_op jit(solution)/shard_map/ppermute | solution.py:285
  180.6 2.4 %collective-permute-done.27.p3 = bf16[8,64,128]{2,1,0:T(8,128)(2,1)S(1)} collective-permute-done((bf16[8,64,128]{2,1,0:T(8,128)(2,1)S(1)}, bf16[8,64,128]{2,1,0:T(8,128)(2,1)S(1)}, u32[]{:S(2)}, u32[]{:S(2)}) %collective-permute-start.27) | collective-permute-done | bytes 131104 | tf_op jit(solution)/shard_map/ppermute | solution.py:285
  187.3 3.1 %collective-permute-done.31 = f32[2,64,128]{2,1,0:T(8,128)S(1)} collective-permute-done((f32[2,64,128]{2,1,0:T(8,128)S(1)}, f32[2,64,128]{2,1,0:T(8,128)S(1)}, u32[]{:S(2)}, u32[]{:S(2)}) %collective-permute-start.31) | collective-permute-done | bytes 65568 | tf_op jit(solution)/shard_map/ppermute | solution.py:289
  190.4 6.9 %collective-permute-start.32 = (f32[64,128]{1,0:T(8,128)S(1)}, f32[64,128]{1,0:T(8,128)S(1)}, u32[]{:S(2)}, u32[]{:S(2)}) collective-permute-start(f32[64,128]{1,0:T(8,128)S(1)} %fusion), channel_id=1, source_target_pairs={{0,32},{32,0},{64,96},{96,64},{128,160},{160,128},{192,224},{224,1... | collective-permute-start | bytes 98312 | tf_op jit(solution)/shard_map/ppermute | solution.py:289
  (118 shorter events, 48.7 us)
Async XLA Ops:
  6.3 7.5 %collective-permute-start.1 = (bf16[8,64,128]{2,1,0:T(8,128)(2,1)}, bf16[8,64,128]{2,1,0:T(8,128)(2,1)S(1)}, u32[]{:S(2)}, u32[]{:S(2)}) collective-permute-start(bf16[8,64,128]{2,1,0:T(8,128)(2,1)} %get-tuple-element.33), channel_id=1, source_target_pairs={{0,8},{1,9},{2,10},{3,11},{4,12},{5,13},{6,14},{7,15},{8,16},{9,17... | collective-permute-start | bytes 393224 | tf_op jit(solution)/shard_map/ppermute | solution.py:285
  6.6 7.2 %collective-permute-start.2 = (bf16[8,64,128]{2,1,0:T(8,128)(2,1)}, bf16[8,64,128]{2,1,0:T(8,128)(2,1)S(1)}, u32[]{:S(2)}, u32[]{:S(2)}) collective-permute-start(bf16[8,64,128]{2,1,0:T(8,128)(2,1)} %get-tuple-element.34), channel_id=1, source_target_pairs={{0,24},{1,25},{2,26},{3,27},{4,28},{5,29},{6,30},{7,31},{8,0},{9,1... | collective-permute-start | bytes 393224 | tf_op jit(solution)/shard_map/ppermute | solution.py:285
  40.8 7.2 %collective-permute-start.5 = (bf16[8,64,128]{2,1,0:T(8,128)(2,1)S(1)}, bf16[8,64,128]{2,1,0:T(8,128)(2,1)S(1)}, u32[]{:S(2)}, u32[]{:S(2)}) collective-permute-start(bf16[8,64,128]{2,1,0:T(8,128)(2,1)S(1)} %all_to_all.31.p0), channel_id=1, source_target_pairs={{0,24},{1,25},{2,26},{3,27},{4,28},{5,29},{6,30},{7,31},{8,0},{9,1... | collective-permute-start | bytes 393224 | tf_op jit(solution)/shard_map/ppermute | solution.py:285
  52.8 11.1 %collective-permute-start.6 = (bf16[32,64,128]{2,1,0:T(8,128)(2,1)}, bf16[32,64,128]{2,1,0:T(8,128)(2,1)}, u32[]{:S(2)}, u32[]{:S(2)}) collective-permute-start(bf16[32,64,128]{2,1,0:T(8,128)(2,1)} %get-tuple-element.36), channel_id=1, source_target_pairs={{0,32},{32,0},{64,96},{96,64},{128,160},{160,128},{192,224},{224,1... | collective-permute-start | bytes 1572872 | tf_op jit(solution)/shard_map/ppermute | solution.py:289
  63.9 36.8 %collective-permute-start.17 = (bf16[64,64,128]{2,1,0:T(8,128)(2,1)}, bf16[64,64,128]{2,1,0:T(8,128)(2,1)}, u32[]{:S(2)}, u32[]{:S(2)}) collective-permute-start(bf16[64,64,128]{2,1,0:T(8,128)(2,1)} %get-tuple-element.45), channel_id=1, source_target_pairs={{0,32},{32,0},{64,96},{96,64},{128,160},{160,128},{192,224},{224,1... | collective-permute-start | bytes 3145736 | tf_op jit(solution)/shard_map/ppermute | solution.py:289
  65.5 6.5 %collective-permute-start.7 = (bf16[8,64,128]{2,1,0:T(8,128)(2,1)S(1)}, bf16[8,64,128]{2,1,0:T(8,128)(2,1)S(1)}, u32[]{:S(2)}, u32[]{:S(2)}) collective-permute-start(bf16[8,64,128]{2,1,0:T(8,128)(2,1)S(1)} %get-tuple-element.38), channel_id=1, source_target_pairs={{0,16},{1,17},{2,18},{3,19},{4,20},{5,21},{6,22},{7,23},{8,24},{9,... | collective-permute-start | bytes 393224 | tf_op jit(solution)/shard_map/ppermute | solution.py:285
  66.0 9.4 %collective-permute-start.8 = (bf16[8,64,128]{2,1,0:T(8,128)(2,1)S(1)}, bf16[8,64,128]{2,1,0:T(8,128)(2,1)S(1)}, u32[]{:S(2)}, u32[]{:S(2)}) collective-permute-start(bf16[8,64,128]{2,1,0:T(8,128)(2,1)S(1)} %get-tuple-element.39), channel_id=1, source_target_pairs={{0,8},{1,9},{2,10},{3,11},{4,12},{5,13},{6,14},{7,15},{8,16},{9,17... | collective-permute-start | bytes 393224 | tf_op jit(solution)/shard_map/ppermute | solution.py:285
  66.5 8.9 %collective-permute-start.9 = (bf16[8,64,128]{2,1,0:T(8,128)(2,1)S(1)}, bf16[8,64,128]{2,1,0:T(8,128)(2,1)S(1)}, u32[]{:S(2)}, u32[]{:S(2)}) collective-permute-start(bf16[8,64,128]{2,1,0:T(8,128)(2,1)S(1)} %get-tuple-element.40), channel_id=1, source_target_pairs={{0,24},{1,25},{2,26},{3,27},{4,28},{5,29},{6,30},{7,31},{8,0},{9,1... | collective-permute-start | bytes 393224 | tf_op jit(solution)/shard_map/ppermute | solution.py:285
  69.7 35.1 %collective-permute-start.13 = (bf16[1,4096,128]{2,1,0:T(8,128)(2,1)}, bf16[1,4096,128]{2,1,0:T(8,128)(2,1)S(1)}, u32[]{:S(2)}, u32[]{:S(2)}) collective-permute-start(bf16[1,4096,128]{2,1,0:T(8,128)(2,1)} %constant_dynamic-slice_fusion.3), channel_id=1, source_target_pairs={{0,32},{32,0},{64,96},{96,64},{128,160},{160,128},{192,224},{224,1... | collective-permute-start | bytes 3145736 | tf_op jit(solution)/shard_map/ppermute | solution.py:289
  86.7 11.9 %all-to-all-start.3 = ((bf16[8,64,128]{2,1,0:T(8,128)(2,1)}), bf16[8,64,128]{2,1,0:T(8,128)(2,1)}, u32[]{:S(2)}, u32[]{:S(2)}) async-start(bf16[8,64,128]{2,1,0:T(8,128)(2,1)} %copy-done.13), calls=%async_computation.3 | async-start | bytes 262144 | tf_op jit(solution)/shard_map/all_to_all | solution.py:294
  98.6 6.4 %collective-permute-start.12 = (bf16[8,64,128]{2,1,0:T(8,128)(2,1)}, bf16[8,64,128]{2,1,0:T(8,128)(2,1)S(1)}, u32[]{:S(2)}, u32[]{:S(2)}) collective-permute-start(bf16[8,64,128]{2,1,0:T(8,128)(2,1)} %all-to-all-done.3.p0), channel_id=1, source_target_pairs={{0,24},{1,25},{2,26},{3,27},{4,28},{5,29},{6,30},{7,31},{8,0},{9,1... | collective-permute-start | bytes 393224 | tf_op jit(solution)/shard_map/ppermute | solution.py:285
  98.6 6.4 %collective-permute-start.11 = (bf16[8,64,128]{2,1,0:T(8,128)(2,1)}, bf16[8,64,128]{2,1,0:T(8,128)(2,1)S(1)}, u32[]{:S(2)}, u32[]{:S(2)}) collective-permute-start(bf16[8,64,128]{2,1,0:T(8,128)(2,1)} %all-to-all-done.3.p0), channel_id=1, source_target_pairs={{0,16},{1,17},{2,18},{3,19},{4,20},{5,21},{6,22},{7,23},{8,24},{9,... | collective-permute-start | bytes 393224 | tf_op jit(solution)/shard_map/ppermute | solution.py:285
  100.8 13.1 %collective-permute-start.15 = (s32[1,4]{1,0:T(1,128)S(1)}, s32[1,4]{1,0:T(1,128)S(1)}, u32[]{:S(2)}, u32[]{:S(2)}) collective-permute-start(s32[1,4]{1,0:T(1,128)S(1)} %slice_bitcast_fusion.2), channel_id=1, source_target_pairs={{0,64},{32,96},{64,0},{96,32},{128,192},{160,224},{192,128},{224,1... | collective-permute-start | bytes 56 | tf_op jit(solution)/shard_map/ppermute | solution.py:289
  104.8 39.2 %collective-permute-start.18 = (bf16[32,64,128]{2,1,0:T(8,128)(2,1)S(1)}, bf16[32,64,128]{2,1,0:T(8,128)(2,1)S(1)}, u32[]{:S(2)}, u32[]{:S(2)}) collective-permute-start(bf16[32,64,128]{2,1,0:T(8,128)(2,1)S(1)} %get-tuple-element.47), channel_id=1, source_target_pairs={{0,64},{32,96},{64,0},{96,32},{128,192},{160,224},{192,128},{224,1... | collective-permute-start | bytes 1572872 | tf_op jit(solution)/shard_map/ppermute | solution.py:289
  111.7 68.0 %collective-permute-start.30 = (bf16[1,4096,128]{2,1,0:T(8,128)(2,1)S(1)}, bf16[1,4096,128]{2,1,0:T(8,128)(2,1)S(1)}, u32[]{:S(2)}, u32[]{:S(2)}) collective-permute-start(bf16[1,4096,128]{2,1,0:T(8,128)(2,1)S(1)} %get-tuple-element.57), channel_id=1, source_target_pairs={{0,96},{32,64},{64,32},{96,0},{128,224},{160,192},{192,160},{224,1... | collective-permute-start | bytes 3145736 | tf_op jit(solution)/shard_map/ppermute | solution.py:289
  113.1 24.9 %collective-permute-start.19 = (bf16[4,64,128]{2,1,0:T(8,128)(2,1)S(1)}, bf16[4,64,128]{2,1,0:T(8,128)(2,1)S(1)}, u32[]{:S(2)}, u32[]{:S(2)}) collective-permute-start(bf16[4,64,128]{2,1,0:T(8,128)(2,1)S(1)} %get-tuple-element.48.refs_0_), channel_id=1, source_target_pairs={{0,64},{32,96},{64,0},{96,32},{128,192},{160,224},{192,128},{224,1... | collective-permute-start | bytes 196616 | tf_op jit(solution)/shard_map/ppermute | solution.py:289
  113.9 29.2 %collective-permute-start.16 = (s32[2,4]{1,0:T(2,128)S(1)}, s32[2,4]{1,0:T(2,128)S(1)}, u32[]{:S(2)}, u32[]{:S(2)}) collective-permute-start(s32[2,4]{1,0:T(2,128)S(1)} %pad_add_fusion.1), channel_id=1, source_target_pairs={{0,32},{32,0},{64,96},{96,64},{128,160},{160,128},{192,224},{224,1... | collective-permute-start | bytes 104 | tf_op jit(solution)/shard_map/ppermute | solution.py:289
  114.6 28.5 %collective-permute-start.20 = (bf16[4,64,128]{2,1,0:T(8,128)(2,1)S(1)}, bf16[4,64,128]{2,1,0:T(8,128)(2,1)S(1)}, u32[]{:S(2)}, u32[]{:S(2)}) collective-permute-start(bf16[4,64,128]{2,1,0:T(8,128)(2,1)S(1)} %get-tuple-element.48.refs_0_), channel_id=1, source_target_pairs={{0,32},{32,0},{64,96},{96,64},{128,160},{160,128},{192,224},{224,1... | collective-permute-start | bytes 196616 | tf_op jit(solution)/shard_map/ppermute | solution.py:289
  145.0 7.2 %collective-permute-start.22 = (bf16[8,64,128]{2,1,0:T(8,128)(2,1)S(1)}, bf16[8,64,128]{2,1,0:T(8,128)(2,1)S(1)}, u32[]{:S(2)}, u32[]{:S(2)}) collective-permute-start(bf16[8,64,128]{2,1,0:T(8,128)(2,1)S(1)} %get-tuple-element.50), channel_id=1, source_target_pairs={{0,16},{1,17},{2,18},{3,19},{4,20},{5,21},{6,22},{7,23},{8,24},{9,... | collective-permute-start | bytes 393224 | tf_op jit(solution)/shard_map/ppermute | solution.py:285
  148.6 32.0 %collective-permute-start.29 = (bf16[1,4096,128]{2,1,0:T(8,128)(2,1)S(1)}, bf16[1,4096,128]{2,1,0:T(8,128)(2,1)S(1)}, u32[]{:S(2)}, u32[]{:S(2)}) collective-permute-start(bf16[1,4096,128]{2,1,0:T(8,128)(2,1)S(1)} %get-tuple-element.58), channel_id=1, source_target_pairs={{0,64},{32,96},{64,0},{96,32},{128,192},{160,224},{192,128},{224,1... | collective-permute-start | bytes 3145736 | tf_op jit(solution)/shard_map/ppermute | solution.py:289
  148.8 31.8 %collective-permute-start.28 = (bf16[1,4096,128]{2,1,0:T(8,128)(2,1)S(1)}, bf16[1,4096,128]{2,1,0:T(8,128)(2,1)S(1)}, u32[]{:S(2)}, u32[]{:S(2)}) collective-permute-start(bf16[1,4096,128]{2,1,0:T(8,128)(2,1)S(1)} %get-tuple-element.59), channel_id=1, source_target_pairs={{0,32},{32,0},{64,96},{96,64},{128,160},{160,128},{192,224},{224,1... | collective-permute-start | bytes 3145736 | tf_op jit(solution)/shard_map/ppermute | solution.py:289
  149.7 6.3 %collective-permute-start.23 = (bf16[8,64,128]{2,1,0:T(8,128)(2,1)S(1)}, bf16[8,64,128]{2,1,0:T(8,128)(2,1)S(1)}, u32[]{:S(2)}, u32[]{:S(2)}) collective-permute-start(bf16[8,64,128]{2,1,0:T(8,128)(2,1)S(1)} %get-tuple-element.51), channel_id=1, source_target_pairs={{0,8},{1,9},{2,10},{3,11},{4,12},{5,13},{6,14},{7,15},{8,16},{9,17... | collective-permute-start | bytes 393224 | tf_op jit(solution)/shard_map/ppermute | solution.py:285
  179.7 6.4 %collective-permute-start.25 = (bf16[8,64,128]{2,1,0:T(8,128)(2,1)S(1)}, bf16[8,64,128]{2,1,0:T(8,128)(2,1)S(1)}, u32[]{:S(2)}, u32[]{:S(2)}) collective-permute-start(bf16[8,64,128]{2,1,0:T(8,128)(2,1)S(1)} %all_to_all.34.p0), channel_id=1, source_target_pairs={{0,8},{1,9},{2,10},{3,11},{4,12},{5,13},{6,14},{7,15},{8,16},{9,17... | collective-permute-start | bytes 393224 | tf_op jit(solution)/shard_map/ppermute | solution.py:285
  190.4 7.8 %collective-permute-start.32 = (f32[64,128]{1,0:T(8,128)S(1)}, f32[64,128]{1,0:T(8,128)S(1)}, u32[]{:S(2)}, u32[]{:S(2)}) collective-permute-start(f32[64,128]{1,0:T(8,128)S(1)} %fusion), channel_id=1, source_target_pairs={{0,32},{32,0},{64,96},{96,64},{128,160},{160,128},{192,224},{224,1... | collective-permute-start | bytes 98312 | tf_op jit(solution)/shard_map/ppermute | solution.py:289
  (31 other events, 392.6 us)

commit v3 on v2

--- a/solution.py
+++ b/solution.py
@@ -87,7 +87,7 @@
         out_specs=[pl.BlockSpec((blocks // outs, height, q), lambda i: (0, 0, 0))] * outs,
         out_shape=[jax.ShapeDtypeStruct((blocks // outs, height, q), BF16)] * outs,
         scratch_shapes=[pltpu.VMEM((blocks, height, q), F32)],
-        compiler_params=pltpu.CompilerParams(vmem_limit_bytes=61 * 2**20)
+        compiler_params=pltpu.CompilerParams(vmem_limit_bytes=52 * 2**20)
         if level == 0
         else PARAMS,
         cost_estimate=pl.CostEstimate(
@@ -238,9 +238,9 @@
     )(mine, other, panels)
 
 
-def merge_kernel(rows, a, b, *refs):
+def merge_kernel(*refs):
     place = here()
-    terms, outs, total = refs[:4], refs[4:8], refs[8]
+    rows, (a, b), terms, outs, total = refs[:4], refs[4:6], refs[6:10], refs[10:14], refs[14]
     blocks = a.shape[0]
     members = ALONG_X * DEPTH
 
@@ -251,7 +251,7 @@
 
     for source, term in enumerate(terms):
         for t in range(term.shape[0]):
-            entry = rows[source, t]
+            entry = rows[source][2, 0, t]
 
             @pl.when(lax.div(entry, members) == place[3])
             def _():
@@ -266,14 +266,31 @@
     piece = jax.ShapeDtypeStruct((DEPTH, *a.shape[1:]), BF16)
     return pl.pallas_call(
         merge_kernel,
-        in_specs=[SCALARS] + [WHOLE] * 6,
+        in_specs=[SCALARS] * 4 + [WHOLE] * 6,
         out_specs=[WHOLE] * ALONG_X,
         out_shape=[piece] * ALONG_X,
         scratch_shapes=[pltpu.VMEM(a.shape, F32)],
         compiler_params=PARAMS,
         cost_estimate=pl.CostEstimate(flops=a.size, bytes_accessed=6 * a.size, transcendentals=0),
         name="merge",
-    )(rows, a, b, *terms)
+    )(*rows, a, b, *terms)
+
+
+def finish_kernel(first, second, a, b, c, d, out):
+    out[0, 0] = first[...]
+    out[1, 0] = second[...]
+    out[2, 0] = (a[...] + b[...] + c[...] + d[...]).astype(BF16)
+
+
+def finish(*args):
+    return pl.pallas_call(
+        finish_kernel,
+        in_specs=[WHOLE] * 6,
+        out_specs=WHOLE,
+        out_shape=jax.ShapeDtypeStruct((3, 1, *args[0].shape), BF16),
+        compiler_params=PARAMS,
+        name="finish",
+    )(*args)
 
 
 def along_x(value, step):
@@ -320,7 +337,8 @@
     for part in arrived:
         total = total + part.astype(F32)
     total = total.astype(BF16)
-    return residual_copies(over_z(total), right, level)
+    summed = over_z(total)
+    return residual_copies(summed, right, level)
 
 
 def gather(copies):
@@ -355,11 +373,9 @@
     top_others = []
     for mask in (1, 2, 3):
         top_others.append(swapped(turned(inverse_top, quarter ^ mask), mask))
-    rows_mine = source[2]
-    rows_high = swapped(rows_mine, 2)
-    rows_two = jnp.concatenate([rows_mine, rows_high])
-    rows_core = swapped(rows_two, 1)
-    rows_all = jnp.concatenate([rows_two, rows_core])
+    rows_all = [source]
+    for mask in (2, 1, 3):
+        rows_all.append(swapped(source, mask))
 
     (base_mid,) = leaf_sums(1, rows, leaf_solution, leaf_panels)
     (base_top,) = leaf_sums(2, rows, leaf_solution, leaf_panels)
@@ -380,11 +396,11 @@
     terms_core = swapped(terms, 1)
     terms_both = swapped(terms_high, 1)
     pieces = merge(rows_all, stay, arrived, [terms, terms_high, terms_core, terms_both])
+    pieces, top_others = lax.optimization_barrier((pieces, top_others))
     copies = collect(pieces, right_sides, 2)
     mine, by_core, by_high, by_both = partials(gather(copies), inverse_top, top_others, F32)
-    pair = swapped(jnp.stack([by_high, by_both]), 2)
-    third = (mine + pair[0] + swapped(by_core + pair[1], 1)).astype(BF16)
-    return jnp.stack([first, second, third])[:, None]
+    arrived = [swapped(by_high, 2), swapped(by_both, 3), swapped(by_core, 1)]
+    return finish(first, second, mine, *arrived)
 
 
 def solution(mesh):

time: 200 us -> 213 us (1.065)
  local copies, waits for them, and re-layouts: 9.02 us -> 15.6 us
  blocking collectives: 57.3 us -> 50.8 us
  starting transfers between devices: 55.3 us -> 60.3 us
  waiting for transfers between devices: 58.3 us -> 63.2 us
  Pallas kernels: 16.9 us -> 19.7 us
    all_to_all x5 -> x4, blocking collectives: 57.3 us -> 50.8 us  [over_z(): lax.all_to_all(pieces, 'member', 0, 0, axis_index_groups=groups, tiled=True)]
    ppermute x18, waiting for transfers between devices: 22.2 us -> 27.9 us  [along_x(): return lax.ppermute(value, 'member', pairs)]
    dynamic_slice x2, local copies, waits for them, and re-layouts: 1.24 us -> 6.1 us  [turned(): return lax.dynamic_slice_in_dim(inverse, at * span, span, 1)]
    all_to_all x1 -> x2, starting transfers between devices: 4 us -> 8.56 us  [over_z(): lax.all_to_all(pieces, 'member', 0, 0, axis_index_groups=groups, tiled=True)]
    ppermute x15 -> x17, waiting for transfers between devices: 28.3 us -> 25 us  [swapped(): lax.ppermute(value, 'group', [(g, g ^ mask) for g in range(lax.axis_size(...]
    unnamed x42 -> x46, local copies, waits for them, and re-layouts: 7.13 us -> 9.55 us
    all_to_all x1 -> x2, waiting for transfers between devices: 7.9 us -> 10.3 us  [over_z(): lax.all_to_all(pieces, 'member', 0, 0, axis_index_groups=groups, tiled=True)]
    ppermute x15 -> x17, starting transfers between devices: 28.8 us -> 30.5 us  [swapped(): lax.ppermute(value, 'group', [(g, g ^ mask) for g in range(lax.axis_size(...]
  transfers between devices with their start and end apart: 34 -> 37, of which waited for: 17 -> 23; matrix products, arithmetic and copies ran while one was open for 1% -> 4% of each run, Pallas kernels for 6% -> 5%
where the time goes in v3:
time: 213 us; the launch traced here: 212 us
  waiting for transfers between devices  63.2 us (30%)
  starting transfers between devices  60.3 us (28%)
  blocking collectives  50.8 us (24%)
  Pallas kernels  19.7 us (9%)
  local copies, waits for them, and re-layouts  15.6 us (7%)
    all_to_all x4, blocking collectives, over_z(): lax.all_to_all(pieces, 'member', 0, 0, axis_index_groups=groups, tiled=True)  50.8 us
    ppermute x17, starting transfers between devices, swapped(): lax.ppermute(value, 'group', [(g, g ^ mask) for g in range(lax.axis_size(...  30.5 us
    ppermute x18, waiting for transfers between devices, along_x(): return lax.ppermute(value, 'member', pairs)  27.9 us
    ppermute x17, waiting for transfers between devices, swapped(): lax.ppermute(value, 'group', [(g, g ^ mask) for g in range(lax.axis_size(...  25 us
    ppermute x18, starting transfers between devices, along_x(): return lax.ppermute(value, 'member', pairs)  21.3 us
    all_to_all x2, waiting for transfers between devices, over_z(): lax.all_to_all(pieces, 'member', 0, 0, axis_index_groups=groups, tiled=True)  10.3 us
    unnamed x46, local copies, waits for them, and re-layouts  9.55 us
    all_to_all x2, starting transfers between devices, over_z(): lax.all_to_all(pieces, 'member', 0, 0, axis_index_groups=groups, tiled=True)  8.56 us
  transfers between devices with their start and end apart: 37, of which 23 were waited for; matrix products, arithmetic and copies ran while one was open for 4% of the time, Pallas kernels for 5%

profile of v3, /device:TPU:1, one launch (start us, length us, event | category | flops | bytes accessed | tf_op | source)
XLA Modules:
  0.0 211.9 jit_solution(942652366170458601)
XLA Ops:
  3.6 3.6 %collective-permute-start = (bf16[8,64,128]{2,1,0:T(8,128)(2,1)S(1)}, bf16[8,64,128]{2,1,0:T(8,128)(2,1)S(1)}, u32[]{:S(2)}, u32[]{:S(2)}) collective-permute-start(bf16[8,64,128]{2,1,0:T(8,128)(2,1)S(1)} %get-tuple-element.39), channel_id=1, source_target_pairs={{0,16},{1,17},{2,18},{3,19},{4,20},{5,21},{6,22},{7,23},{8,24},{9,... | collective-permute-start | bytes 393224 | tf_op jit(solution)/shard_map/ppermute | solution.py:302
  7.6 2.4 %collective-permute-start.2 = (bf16[8,64,128]{2,1,0:T(8,128)(2,1)S(1)}, bf16[8,64,128]{2,1,0:T(8,128)(2,1)S(1)}, u32[]{:S(2)}, u32[]{:S(2)}) collective-permute-start(bf16[8,64,128]{2,1,0:T(8,128)(2,1)S(1)} %get-tuple-element.41), channel_id=1, source_target_pairs={{0,24},{1,25},{2,26},{3,27},{4,28},{5,29},{6,30},{7,31},{8,0},{9,1... | collective-permute-start | bytes 393224 | tf_op jit(solution)/shard_map/ppermute | solution.py:302
  9.9 4.6 %collective-permute-done.1 = bf16[8,64,128]{2,1,0:T(8,128)(2,1)S(1)} collective-permute-done((bf16[8,64,128]{2,1,0:T(8,128)(2,1)S(1)}, bf16[8,64,128]{2,1,0:T(8,128)(2,1)S(1)}, u32[]{:S(2)}, u32[]{:S(2)}) %collective-permute-start.1) | collective-permute-done | bytes 131104 | tf_op jit(solution)/shard_map/ppermute | solution.py:302
  14.6 15.4 %all_to_all.30.arrived = bf16[8,64,128]{2,1,0:T(8,128)(2,1)S(1)} all-to-all(bf16[8,64,128]{2,1,0:T(8,128)(2,1)S(1)} %add_convert_fusion.2), channel_id=1, replica_groups={{0,1,2,3,4,5,6,7},{8,9,10,11,12,13,14,15},{16,17,18,19,20,21,22,23},{24..., dimensions={0} | all-to-all | bytes 262144 | tf_op jit(solution)/shard_map/all_to_all | solution.py:311
  30.1 10.5 %all_to_all.31.p0 = bf16[8,64,128]{2,1,0:T(8,128)(2,1)S(1)} all-to-all(bf16[8,64,128]{2,1,0:T(8,128)(2,1)S(1)} %shard_map.92), channel_id=1, replica_groups={{0,1,2,3,4,5,6,7},{8,9,10,11,12,13,14,15},{16,17,18,19,20,21,22,23},{24..., dimensions={0} | all-to-all | bytes 262144 | tf_op jit(solution)/shard_map/all_to_all | solution.py:311
  52.7 5.4 %collective-permute-start.6 = (bf16[32,64,128]{2,1,0:T(8,128)(2,1)}, bf16[32,64,128]{2,1,0:T(8,128)(2,1)}, u32[]{:S(2)}, u32[]{:S(2)}) collective-permute-start(bf16[32,64,128]{2,1,0:T(8,128)(2,1)} %get-tuple-element.43), channel_id=1, source_target_pairs={{0,32},{32,0},{64,96},{96,64},{128,160},{160,128},{192,224},{224,1... | collective-permute-start | bytes 1572872 | tf_op jit(solution)/shard_map/ppermute | solution.py:306
  64.4 2.2 %collective-permute-start.9 = (bf16[8,64,128]{2,1,0:T(8,128)(2,1)}, bf16[8,64,128]{2,1,0:T(8,128)(2,1)}, u32[]{:S(2)}, u32[]{:S(2)}) collective-permute-start(bf16[8,64,128]{2,1,0:T(8,128)(2,1)} %get-tuple-element.47), channel_id=1, source_target_pairs={{0,24},{1,25},{2,26},{3,27},{4,28},{5,29},{6,30},{7,31},{8,0},{9,1... | collective-permute-start | bytes 393224 | tf_op jit(solution)/shard_map/ppermute | solution.py:302
  66.5 2.3 %constant_dynamic-slice_fusion.3 = bf16[1,4096,128]{2,1,0:T(8,128)(2,1)} fusion(bf16[1,8192,128]{2,1,0:T(8,128)(2,1)} %refs_0_.4, s32[]{:T(128)S(6)} %select_n.12), kind=kLoop, calls=%fused_computation.6 | loop fusion | bytes 2097156 | tf_op jit(solution)/shard_map/dynamic_slice | solution.py:368
  73.4 2.3 %shard_map.100 = (bf16[64,64,128]{2,1,0:T(8,128)(2,1)S(1)}, bf16[64,64,128]{2,1,0:T(8,128)(2,1)}) custom-call(s32[3,1,4]{2,1,0:T(1,128)S(1)} %bitcast.6, bf16[64,128]{1,0:T(8,128)(2,1)S(1)} %shard_map.93.value.first, bf16[1,3,4,128,128]{4,3,2,1,0:T(8,128)(2,1)S(1)} %copy-done.3, bf16[128,64,128]{2,1,0:T(8,128)(2,1)S(1)} %shard_map.99.base), custom_call_target="tpu_custom_call" | custom-call | flops 8388608 | bytes 4194304 | tf_op jit(solution)/shard_map/pallas_call | solution.py:164
  78.5 4.0 %all-to-all-start.2 = ((bf16[8,64,128]{2,1,0:T(8,128)(2,1)}), bf16[8,64,128]{2,1,0:T(8,128)(2,1)}, u32[]{:S(2)}, u32[]{:S(2)}) async-start(bf16[8,64,128]{2,1,0:T(8,128)(2,1)} %add_convert_fusion.1), calls=%async_computation.2 | async-start | bytes 262144 | tf_op jit(solution)/shard_map/all_to_all | solution.py:311
  82.5 3.8 %constant_dynamic-slice_fusion = (bf16[1,4096,128]{2,1,0:T(8,128)(2,1)}, bf16[1,4096,128]{2,1,0:T(8,128)(2,1)}, bf16[1,4096,128]{2,1,0:T(8,128)(2,1)}) fusion(bf16[1,16384,128]{2,1,0:T(8,128)(2,1)} %refs_0_.5, s32[]{:T(128)S(6)} %select_n.15, s32[]{:T(128)S(6)} %select_n.14, s32[]{:T(128)S(6)} %select_n.13), kind=kLoop, calls=%fused_computation.3 | loop fusion | bytes 6291468 | tf_op jit(solution)/shard_map/dynamic_slice | solution.py:368
  88.4 2.2 %all-to-all-done.2.arrived = bf16[8,64,128]{2,1,0:T(8,128)(2,1)} async-done(((bf16[8,64,128]{2,1,0:T(8,128)(2,1)}), bf16[8,64,128]{2,1,0:T(8,128)(2,1)}, u32[]{:S(2)}, u32[]{:S(2)}) %all-to-all-start.2) | async-done | bytes 131104 | tf_op jit(solution)/shard_map/all_to_all | solution.py:311
  93.0 4.6 %all-to-all-start.3 = ((bf16[8,64,128]{2,1,0:T(8,128)(2,1)}), bf16[8,64,128]{2,1,0:T(8,128)(2,1)}, u32[]{:S(2)}, u32[]{:S(2)}) async-start(bf16[8,64,128]{2,1,0:T(8,128)(2,1)} %copy-done.11), calls=%async_computation.3 | async-start | bytes 262144 | tf_op jit(solution)/shard_map/all_to_all | solution.py:311
  97.5 8.1 %all-to-all-done.3.p0 = bf16[8,64,128]{2,1,0:T(8,128)(2,1)} async-done(((bf16[8,64,128]{2,1,0:T(8,128)(2,1)}), bf16[8,64,128]{2,1,0:T(8,128)(2,1)}, u32[]{:S(2)}, u32[]{:S(2)}) %all-to-all-start.3) | async-done | bytes 131104 | tf_op jit(solution)/shard_map/all_to_all | solution.py:311
  111.4 4.1 %collective-permute-done.11.p2 = bf16[8,64,128]{2,1,0:T(8,128)(2,1)S(1)} collective-permute-done((bf16[8,64,128]{2,1,0:T(8,128)(2,1)}, bf16[8,64,128]{2,1,0:T(8,128)(2,1)S(1)}, u32[]{:S(2)}, u32[]{:S(2)}) %collective-permute-start.11) | collective-permute-done | bytes 131104 | tf_op jit(solution)/shard_map/ppermute | solution.py:302
  116.6 4.2 %collective-permute-done.10.p1 = bf16[8,64,128]{2,1,0:T(8,128)(2,1)S(1)} collective-permute-done((bf16[8,64,128]{2,1,0:T(8,128)(2,1)}, bf16[8,64,128]{2,1,0:T(8,128)(2,1)S(1)}, u32[]{:S(2)}, u32[]{:S(2)}) %collective-permute-start.10) | collective-permute-done | bytes 131104 | tf_op jit(solution)/shard_map/ppermute | solution.py:302
  122.6 5.5 %collective-permute-start.14 = (f32[64,128]{1,0:T(8,128)S(1)}, f32[64,128]{1,0:T(8,128)S(1)}, u32[]{:S(2)}, u32[]{:S(2)}) collective-permute-start(f32[64,128]{1,0:T(8,128)S(1)} %get-tuple-element.49), channel_id=1, source_target_pairs={{0,32},{32,0},{64,96},{96,64},{128,160},{160,128},{192,224},{224,1... | collective-permute-start | bytes 98312 | tf_op jit(solution)/shard_map/ppermute | solution.py:306
  131.2 14.6 %collective-permute-done.17.refs_3_ = s32[3,1,4]{2,1,0:T(1,128)S(1)} collective-permute-done((s32[3,1,4]{2,1,0:T(1,128)S(1)}, s32[3,1,4]{2,1,0:T(1,128)S(1)}, u32[]{:S(2)}, u32[]{:S(2)}) %collective-permute-start.17) | collective-permute-done | bytes 80 | tf_op jit(solution)/shard_map/ppermute | solution.py:306
  159.7 2.7 %collective-permute-start.28 = (bf16[8,64,128]{2,1,0:T(8,128)(2,1)S(1)}, bf16[8,64,128]{2,1,0:T(8,128)(2,1)S(1)}, u32[]{:S(2)}, u32[]{:S(2)}) collective-permute-start(bf16[8,64,128]{2,1,0:T(8,128)(2,1)S(1)} %get-tuple-element.63), channel_id=1, source_target_pairs={{0,24},{1,25},{2,26},{3,27},{4,28},{5,29},{6,30},{7,31},{8,0},{9,1... | collective-permute-start | bytes 393224 | tf_op jit(solution)/shard_map/ppermute | solution.py:302
  164.5 3.5 %collective-permute-done.27 = bf16[8,64,128]{2,1,0:T(8,128)(2,1)S(1)} collective-permute-done((bf16[8,64,128]{2,1,0:T(8,128)(2,1)S(1)}, bf16[8,64,128]{2,1,0:T(8,128)(2,1)S(1)}, u32[]{:S(2)}, u32[]{:S(2)}) %collective-permute-start.27) | collective-permute-done | bytes 131104 | tf_op jit(solution)/shard_map/ppermute | solution.py:302
  168.1 14.4 %all_to_all.32.arrived = bf16[8,64,128]{2,1,0:T(8,128)(2,1)S(1)} all-to-all(bf16[8,64,128]{2,1,0:T(8,128)(2,1)S(1)} %add_convert_fusion), channel_id=1, replica_groups={{0,1,2,3,4,5,6,7},{8,9,10,11,12,13,14,15},{16,17,18,19,20,21,22,23},{24..., dimensions={0} | all-to-all | bytes 262144 | tf_op jit(solution)/shard_map/all_to_all | solution.py:311
  182.6 10.4 %all_to_all.33.p0 = bf16[8,64,128]{2,1,0:T(8,128)(2,1)S(1)} all-to-all(bf16[8,64,128]{2,1,0:T(8,128)(2,1)S(1)} %shard_map.102), channel_id=1, replica_groups={{0,1,2,3,4,5,6,7},{8,9,10,11,12,13,14,15},{16,17,18,19,20,21,22,23},{24..., dimensions={0} | all-to-all | bytes 262144 | tf_op jit(solution)/shard_map/all_to_all | solution.py:311
  199.7 2.3 %shard_map.103 = (f32[64,128]{1,0:T(8,128)S(1)}, f32[64,128]{1,0:T(8,128)S(1)}, f32[64,128]{1,0:T(8,128)S(1)}, f32[64,128]{1,0:T(8,128)S(1)}) custom-call(bf16[8,64,128]{2,1,0:T(8,128)(2,1)S(1)} %all_to_all.33.p0, bf16[8,64,128]{2,1,0:T(8,128)(2,1)S(1)} %collective-permute-done.29.p1, bf16[8,64,128]{2,1,0:T(8,128)(2,1)S(1)} %collective-permute-done.30.p2, ...), custom_call_target="tpu_custom_call" | custom-call | flops 268435456 | bytes 4194304 | tf_op jit(solution)/shard_map/pallas_call | solution.py:122
  203.4 5.9 %collective-permute-start.33 = (f32[64,128]{1,0:T(8,128)S(1)}, f32[64,128]{1,0:T(8,128)S(1)}, u32[]{:S(2)}, u32[]{:S(2)}) collective-permute-start(f32[64,128]{1,0:T(8,128)S(1)} %get-tuple-element.69), channel_id=1, source_target_pairs={{0,96},{32,64},{64,32},{96,0},{128,224},{160,192},{192,160},{224,1... | collective-permute-start | bytes 98312 | tf_op jit(solution)/shard_map/ppermute | solution.py:306
  (121 shorter events, 72.6 us)
Async XLA Ops:
  3.6 6.3 %collective-permute-start = (bf16[8,64,128]{2,1,0:T(8,128)(2,1)S(1)}, bf16[8,64,128]{2,1,0:T(8,128)(2,1)S(1)}, u32[]{:S(2)}, u32[]{:S(2)}) collective-permute-start(bf16[8,64,128]{2,1,0:T(8,128)(2,1)S(1)} %get-tuple-element.39), channel_id=1, source_target_pairs={{0,16},{1,17},{2,18},{3,19},{4,20},{5,21},{6,22},{7,23},{8,24},{9,... | collective-permute-start | bytes 393224 | tf_op jit(solution)/shard_map/ppermute | solution.py:302
  7.3 7.3 %collective-permute-start.1 = (bf16[8,64,128]{2,1,0:T(8,128)(2,1)S(1)}, bf16[8,64,128]{2,1,0:T(8,128)(2,1)S(1)}, u32[]{:S(2)}, u32[]{:S(2)}) collective-permute-start(bf16[8,64,128]{2,1,0:T(8,128)(2,1)S(1)} %get-tuple-element.40), channel_id=1, source_target_pairs={{0,8},{1,9},{2,10},{3,11},{4,12},{5,13},{6,14},{7,15},{8,16},{9,17... | collective-permute-start | bytes 393224 | tf_op jit(solution)/shard_map/ppermute | solution.py:302
  7.6 6.9 %collective-permute-start.2 = (bf16[8,64,128]{2,1,0:T(8,128)(2,1)S(1)}, bf16[8,64,128]{2,1,0:T(8,128)(2,1)S(1)}, u32[]{:S(2)}, u32[]{:S(2)}) collective-permute-start(bf16[8,64,128]{2,1,0:T(8,128)(2,1)S(1)} %get-tuple-element.41), channel_id=1, source_target_pairs={{0,24},{1,25},{2,26},{3,27},{4,28},{5,29},{6,30},{7,31},{8,0},{9,1... | collective-permute-start | bytes 393224 | tf_op jit(solution)/shard_map/ppermute | solution.py:302
  43.7 5.8 %collective-permute-start.3 = (bf16[8,64,128]{2,1,0:T(8,128)(2,1)S(1)}, bf16[8,64,128]{2,1,0:T(8,128)(2,1)S(1)}, u32[]{:S(2)}, u32[]{:S(2)}) collective-permute-start(bf16[8,64,128]{2,1,0:T(8,128)(2,1)S(1)} %all_to_all.31.p0), channel_id=1, source_target_pairs={{0,8},{1,9},{2,10},{3,11},{4,12},{5,13},{6,14},{7,15},{8,16},{9,17... | collective-permute-start | bytes 393224 | tf_op jit(solution)/shard_map/ppermute | solution.py:302
  52.7 7.3 %collective-permute-start.6 = (bf16[32,64,128]{2,1,0:T(8,128)(2,1)}, bf16[32,64,128]{2,1,0:T(8,128)(2,1)}, u32[]{:S(2)}, u32[]{:S(2)}) collective-permute-start(bf16[32,64,128]{2,1,0:T(8,128)(2,1)} %get-tuple-element.43), channel_id=1, source_target_pairs={{0,32},{32,0},{64,96},{96,64},{128,160},{160,128},{192,224},{224,1... | collective-permute-start | bytes 1572872 | tf_op jit(solution)/shard_map/ppermute | solution.py:306
  63.5 13.2 %collective-permute-start.7 = (bf16[8,64,128]{2,1,0:T(8,128)(2,1)}, bf16[8,64,128]{2,1,0:T(8,128)(2,1)}, u32[]{:S(2)}, u32[]{:S(2)}) collective-permute-start(bf16[8,64,128]{2,1,0:T(8,128)(2,1)} %get-tuple-element.45), channel_id=1, source_target_pairs={{0,16},{1,17},{2,18},{3,19},{4,20},{5,21},{6,22},{7,23},{8,24},{9,... | collective-permute-start | bytes 393224 | tf_op jit(solution)/shard_map/ppermute | solution.py:302
  63.8 12.9 %collective-permute-start.8 = (bf16[8,64,128]{2,1,0:T(8,128)(2,1)}, bf16[8,64,128]{2,1,0:T(8,128)(2,1)}, u32[]{:S(2)}, u32[]{:S(2)}) collective-permute-start(bf16[8,64,128]{2,1,0:T(8,128)(2,1)} %get-tuple-element.46), channel_id=1, source_target_pairs={{0,8},{1,9},{2,10},{3,11},{4,12},{5,13},{6,14},{7,15},{8,16},{9,17... | collective-permute-start | bytes 393224 | tf_op jit(solution)/shard_map/ppermute | solution.py:302
  64.4 12.3 %collective-permute-start.9 = (bf16[8,64,128]{2,1,0:T(8,128)(2,1)}, bf16[8,64,128]{2,1,0:T(8,128)(2,1)}, u32[]{:S(2)}, u32[]{:S(2)}) collective-permute-start(bf16[8,64,128]{2,1,0:T(8,128)(2,1)} %get-tuple-element.47), channel_id=1, source_target_pairs={{0,24},{1,25},{2,26},{3,27},{4,28},{5,29},{6,30},{7,31},{8,0},{9,1... | collective-permute-start | bytes 393224 | tf_op jit(solution)/shard_map/ppermute | solution.py:302
  68.8 39.6 %collective-permute-start.13 = (bf16[1,4096,128]{2,1,0:T(8,128)(2,1)}, bf16[1,4096,128]{2,1,0:T(8,128)(2,1)}, u32[]{:S(2)}, u32[]{:S(2)}) collective-permute-start(bf16[1,4096,128]{2,1,0:T(8,128)(2,1)} %constant_dynamic-slice_fusion.3), channel_id=1, source_target_pairs={{0,32},{32,0},{64,96},{96,64},{128,160},{160,128},{192,224},{224,1... | collective-permute-start | bytes 3145736 | tf_op jit(solution)/shard_map/ppermute | solution.py:306
  76.7 20.9 %collective-permute-start.18 = (bf16[64,64,128]{2,1,0:T(8,128)(2,1)}, bf16[64,64,128]{2,1,0:T(8,128)(2,1)}, u32[]{:S(2)}, u32[]{:S(2)}) collective-permute-start(bf16[64,64,128]{2,1,0:T(8,128)(2,1)} %get-tuple-element.52), channel_id=1, source_target_pairs={{0,32},{32,0},{64,96},{96,64},{128,160},{160,128},{192,224},{224,1... | collective-permute-start | bytes 3145736 | tf_op jit(solution)/shard_map/ppermute | solution.py:306
  78.5 12.1 %all-to-all-start.2 = ((bf16[8,64,128]{2,1,0:T(8,128)(2,1)}), bf16[8,64,128]{2,1,0:T(8,128)(2,1)}, u32[]{:S(2)}, u32[]{:S(2)}) async-start(bf16[8,64,128]{2,1,0:T(8,128)(2,1)} %add_convert_fusion.1), calls=%async_computation.2 | async-start | bytes 262144 | tf_op jit(solution)/shard_map/all_to_all | solution.py:311
  86.3 71.9 %collective-permute-start.25 = (bf16[1,4096,128]{2,1,0:T(8,128)(2,1)}, bf16[1,4096,128]{2,1,0:T(8,128)(2,1)S(1)}, u32[]{:S(2)}, u32[]{:S(2)}) collective-permute-start(bf16[1,4096,128]{2,1,0:T(8,128)(2,1)} %get-tuple-element.71), channel_id=1, source_target_pairs={{0,96},{32,64},{64,32},{96,0},{128,224},{160,192},{192,160},{224,1... | collective-permute-start | bytes 3145736 | tf_op jit(solution)/shard_map/ppermute | solution.py:306
  88.0 70.2 %collective-permute-start.24 = (bf16[1,4096,128]{2,1,0:T(8,128)(2,1)}, bf16[1,4096,128]{2,1,0:T(8,128)(2,1)}, u32[]{:S(2)}, u32[]{:S(2)}) collective-permute-start(bf16[1,4096,128]{2,1,0:T(8,128)(2,1)} %get-tuple-element.72), channel_id=1, source_target_pairs={{0,64},{32,96},{64,0},{96,32},{128,192},{160,224},{192,128},{224,1... | collective-permute-start | bytes 3145736 | tf_op jit(solution)/shard_map/ppermute | solution.py:306
  88.1 70.1 %collective-permute-start.23 = (bf16[1,4096,128]{2,1,0:T(8,128)(2,1)}, bf16[1,4096,128]{2,1,0:T(8,128)(2,1)}, u32[]{:S(2)}, u32[]{:S(2)}) collective-permute-start(bf16[1,4096,128]{2,1,0:T(8,128)(2,1)} %get-tuple-element.73), channel_id=1, source_target_pairs={{0,32},{32,0},{64,96},{96,64},{128,160},{160,128},{192,224},{224,1... | collective-permute-start | bytes 3145736 | tf_op jit(solution)/shard_map/ppermute | solution.py:306
  93.0 12.7 %all-to-all-start.3 = ((bf16[8,64,128]{2,1,0:T(8,128)(2,1)}), bf16[8,64,128]{2,1,0:T(8,128)(2,1)}, u32[]{:S(2)}, u32[]{:S(2)}) async-start(bf16[8,64,128]{2,1,0:T(8,128)(2,1)} %copy-done.11), calls=%async_computation.3 | async-start | bytes 262144 | tf_op jit(solution)/shard_map/all_to_all | solution.py:311
  108.4 48.7 %collective-permute-start.19 = (bf16[32,64,128]{2,1,0:T(8,128)(2,1)S(1)}, bf16[32,64,128]{2,1,0:T(8,128)(2,1)S(1)}, u32[]{:S(2)}, u32[]{:S(2)}) collective-permute-start(bf16[32,64,128]{2,1,0:T(8,128)(2,1)S(1)} %get-tuple-element.54), channel_id=1, source_target_pairs={{0,64},{32,96},{64,0},{96,32},{128,192},{160,224},{192,128},{224,1... | collective-permute-start | bytes 1572872 | tf_op jit(solution)/shard_map/ppermute | solution.py:306
  110.0 5.5 %collective-permute-start.11 = (bf16[8,64,128]{2,1,0:T(8,128)(2,1)}, bf16[8,64,128]{2,1,0:T(8,128)(2,1)S(1)}, u32[]{:S(2)}, u32[]{:S(2)}) collective-permute-start(bf16[8,64,128]{2,1,0:T(8,128)(2,1)} %all-to-all-done.3.p0), channel_id=1, source_target_pairs={{0,16},{1,17},{2,18},{3,19},{4,20},{5,21},{6,22},{7,23},{8,24},{9,... | collective-permute-start | bytes 393224 | tf_op jit(solution)/shard_map/ppermute | solution.py:302
  122.6 6.4 %collective-permute-start.14 = (f32[64,128]{1,0:T(8,128)S(1)}, f32[64,128]{1,0:T(8,128)S(1)}, u32[]{:S(2)}, u32[]{:S(2)}) collective-permute-start(f32[64,128]{1,0:T(8,128)S(1)} %get-tuple-element.49), channel_id=1, source_target_pairs={{0,32},{32,0},{64,96},{96,64},{128,160},{160,128},{192,224},{224,1... | collective-permute-start | bytes 98312 | tf_op jit(solution)/shard_map/ppermute | solution.py:306
  128.9 16.8 %collective-permute-start.17 = (s32[3,1,4]{2,1,0:T(1,128)S(1)}, s32[3,1,4]{2,1,0:T(1,128)S(1)}, u32[]{:S(2)}, u32[]{:S(2)}) collective-permute-start(s32[3,1,4]{2,1,0:T(1,128)S(1)} %bitcast.7), channel_id=1, source_target_pairs={{0,96},{32,64},{64,32},{96,0},{128,224},{160,192},{192,160},{224,1... | collective-permute-start | bytes 152 | tf_op jit(solution)/shard_map/ppermute | solution.py:306
  158.2 6.3 %collective-permute-start.26 = (bf16[8,64,128]{2,1,0:T(8,128)(2,1)S(1)}, bf16[8,64,128]{2,1,0:T(8,128)(2,1)S(1)}, u32[]{:S(2)}, u32[]{:S(2)}) collective-permute-start(bf16[8,64,128]{2,1,0:T(8,128)(2,1)S(1)} %get-tuple-element.61), channel_id=1, source_target_pairs={{0,16},{1,17},{2,18},{3,19},{4,20},{5,21},{6,22},{7,23},{8,24},{9,... | collective-permute-start | bytes 393224 | tf_op jit(solution)/shard_map/ppermute | solution.py:302
  159.7 8.3 %collective-permute-start.27 = (bf16[8,64,128]{2,1,0:T(8,128)(2,1)S(1)}, bf16[8,64,128]{2,1,0:T(8,128)(2,1)S(1)}, u32[]{:S(2)}, u32[]{:S(2)}) collective-permute-start(bf16[8,64,128]{2,1,0:T(8,128)(2,1)S(1)} %get-tuple-element.62), channel_id=1, source_target_pairs={{0,8},{1,9},{2,10},{3,11},{4,12},{5,13},{6,14},{7,15},{8,16},{9,17... | collective-permute-start | bytes 393224 | tf_op jit(solution)/shard_map/ppermute | solution.py:302
  159.7 8.3 %collective-permute-start.28 = (bf16[8,64,128]{2,1,0:T(8,128)(2,1)S(1)}, bf16[8,64,128]{2,1,0:T(8,128)(2,1)S(1)}, u32[]{:S(2)}, u32[]{:S(2)}) collective-permute-start(bf16[8,64,128]{2,1,0:T(8,128)(2,1)S(1)} %get-tuple-element.63), channel_id=1, source_target_pairs={{0,24},{1,25},{2,26},{3,27},{4,28},{5,29},{6,30},{7,31},{8,0},{9,1... | collective-permute-start | bytes 393224 | tf_op jit(solution)/shard_map/ppermute | solution.py:302
  202.0 7.3 %collective-permute-start.32 = (f32[64,128]{1,0:T(8,128)S(1)}, f32[64,128]{1,0:T(8,128)S(1)}, u32[]{:S(2)}, u32[]{:S(2)}) collective-permute-start(f32[64,128]{1,0:T(8,128)S(1)} %get-tuple-element.68), channel_id=1, source_target_pairs={{0,64},{32,96},{64,0},{96,32},{128,192},{160,224},{192,128},{224,1... | collective-permute-start | bytes 98312 | tf_op jit(solution)/shard_map/ppermute | solution.py:306
  203.4 7.8 %collective-permute-start.33 = (f32[64,128]{1,0:T(8,128)S(1)}, f32[64,128]{1,0:T(8,128)S(1)}, u32[]{:S(2)}, u32[]{:S(2)}) collective-permute-start(f32[64,128]{1,0:T(8,128)S(1)} %get-tuple-element.69), channel_id=1, source_target_pairs={{0,96},{32,64},{64,32},{96,0},{128,224},{160,192},{192,160},{224,1... | collective-permute-start | bytes 98312 | tf_op jit(solution)/shard_map/ppermute | solution.py:306
  (36 other events, 490.8 us)
